TPU v7x, 32 devices: a whole 2x2x4 slice. The times are simulated.
32 devices in a mesh: outer: 4 (over y, core), inner: 8 (over z, x).
Axes of the slice: x: 2, y: 2, z: 4, core: 2. Of those that a mesh axis runs over, the one named last changes fastest.
Arguments:
- amplitudes: float32 [2, 8388608], P(None, ('outer', 'inner')), may hold values from -200 to 200
Outputs:
- transformed: float32 [2, 8388608], P(None, ('outer', 'inner'))
- checks: float32 [3], replicated
All inputs are finite; a program needn't handle non-finite values.
Results may differ from a plain program's by a relative error of at most 0.00007.
Values sent between devices are 32-bit elements; how exact they have to be, the bound alone decides.
A program may use at most 64 MiB of HBM per device.

v0:
```python
import functools
import math

import jax
import jax.numpy as jnp
import numpy as np
from jax import lax
from jax.experimental import pallas as pl
from jax.experimental.pallas import tpu as pltpu
from jax.sharding import PartitionSpec as P

WINDOW = 9
STEPS = 8
COLUMNS = 2**WINDOW
LANES = 128
SUB = 8
RADIX = COLUMNS // LANES
MESH = pl.DeviceIdType.MESH


def rev(value, count):
    out = 0
    for bit in range(count):
        out |= (value >> bit & 1) << (count - 1 - bit)
    return out


def split_bf16(values):
    high = values.astype(jnp.bfloat16)
    return high, (values - high.astype(np.float32)).astype(jnp.bfloat16)


def tables(rows_count, n_devices):
    f = np.arange(COLUMNS).reshape(LANES, RADIX).T
    lane = np.arange(LANES)
    ang = (f[:, :, None] * lane) % COLUMNS * (2.0 * np.pi / COLUMNS)
    c, s = np.cos(ang) / math.sqrt(COLUMNS), np.sin(ang) / math.sqrt(COLUMNS)
    table = np.stack([np.concatenate([c, -s], -1), np.concatenate([s, c], -1)], 2)
    table = table.reshape(RADIX, 2 * LANES, 2 * LANES).astype(np.float32)
    fa = f * (2.0 * np.pi / COLUMNS)
    cf = np.zeros((RADIX, SUB, LANES, 2), np.float32)
    cf[:, 0, :, 0], cf[:, 0, :, 1] = np.cos(fa), np.sin(fa)
    cf[:, 1, :, 0], cf[:, 1, :, 1] = -np.sin(fa), np.cos(fa)
    cf = cf.reshape(RADIX, SUB, 2 * LANES)
    bits = rows_count.bit_length() - 1
    ra = np.array([rev(r, bits) for r in range(rows_count)]) * (2.0 * np.pi / (rows_count * COLUMNS))
    cr = np.zeros((SUB, rows_count), np.float32)
    cr[0], cr[1] = np.cos(ra), np.sin(ra)
    return table, cf, cr


def swap_sublanes(v):
    at = lax.broadcasted_iota(jnp.int32, v.shape, 1)
    up, down = pltpu.roll(v, 5, 1), pltpu.roll(v, 3, 1)
    v = jnp.where((at == 1) | (at == 3), up, v)
    return jnp.where((at == 4) | (at == 6), down, v)


def kernel(n_outer, n_inner, rows_count, total_len, x_hbm, th_hbm, tl_hbm, cf_hbm, cr_hbm, out_hbm, tot_ref, fac_ref,
           x_ref, th_ref, tl_ref, cf_ref, cr_ref, out_ref, sendbuf, recv, stat_out, stats, send_sem, recv_sem, own_sem, ssend_sem, srecv_sem, load_sem, out_sem):
    n_devices = n_outer * n_inner
    obits, ibits = n_outer.bit_length() - 1, n_inner.bit_length() - 1
    o, i = lax.axis_index("outer"), lax.axis_index("inner")
    me = o * n_inner + i
    slot = 0
    odelta, idelta = [], []
    for k in range(obits):
        bit = o // 2**k % 2
        slot = slot + bit * 2 ** (obits - 1 - k)
        odelta.append((1 - 2 * bit) * 2**k)
    for k in range(ibits):
        bit = i // 2**k % 2
        slot = slot + bit * 2 ** (ibits - 1 - k) * n_outer
        idelta.append((1 - 2 * bit) * 2**k)

    def peer(mo, mi):
        po, pi = o, i
        for k in range(obits):
            if mo >> k & 1:
                po = po + odelta[k]
        for k in range(ibits):
            if mi >> k & 1:
                pi = pi + idelta[k]
        return po, pi

    masks = [(mo, mi) for mi in range(n_inner) for mo in range(n_outer) if mo or mi]
    peers = [peer(mo, mi) for mo, mi in masks]

    barrier = pltpu.get_barrier_semaphore()
    for p in peers:
        pl.semaphore_signal(barrier, inc=1, device_id=p, device_id_type=MESH)

    loads = [pltpu.make_async_copy(src, dst, load_sem.at[k]) for k, (src, dst) in enumerate(
        [(x_hbm, x_ref), (th_hbm, th_ref), (tl_hbm, tl_ref), (cf_hbm, cf_ref), (cr_hbm, cr_ref)])]
    for load in loads:
        load.start()

    groups = rows_count // LANES
    block = SUB * groups

    def data_copy(chunk, n):
        po, pi = peers[n]
        e = po * n_inner + pi
        return pltpu.make_async_remote_copy(
            src_ref=sendbuf.at[pl.ds(pl.multiple_of((chunk * n_devices + e) * block, block), block)],
            dst_ref=recv.at[pl.ds(pl.multiple_of((chunk * n_devices + slot) * block, block), block)],
            send_sem=send_sem.at[chunk, n], recv_sem=recv_sem.at[chunk, n],
            device_id=peers[n], device_id_type=MESH)

    def own_copy(chunk):
        return pltpu.make_async_copy(
            sendbuf.at[pl.ds(pl.multiple_of((chunk * n_devices + me) * block, block), block)],
            recv.at[pl.ds(pl.multiple_of((chunk * n_devices + slot) * block, block), block)],
            own_sem.at[chunk])

    def stat_copy(n):
        return pltpu.make_async_remote_copy(
            src_ref=stat_out, dst_ref=stats.at[slot],
            send_sem=ssend_sem.at[n], recv_sem=srecv_sem.at[n],
            device_id=peers[n], device_id_type=MESH)

    def send(chunk):
        for n in range(len(peers)):
            data_copy(chunk, n).start()
        own_copy(chunk).start()

    dims = (((1,), (1,)), ((), ()))
    loads[0].wait()
    parts = [[x_ref[pl.ds(2 * ct + s, rows_count, stride=2 * RADIX), :] for s in range(2)] for ct in range(RADIX)]
    (x0r, x0i), (x1r, x1i), (x2r, x2i), (x3r, x3i) = parts
    ar, ai, br, bi = x0r + x2r, x0i + x2i, x0r - x2r, x0i - x2i
    cr_, ci_, dr, di = x1r + x3r, x1i + x3i, x1r - x3r, x1i - x3i
    mixed = [(ar + cr_, ai + ci_), (br - di, bi + dr), (ar - cr_, ai - ci_), (br + di, bi - dr)]
    squares = jnp.zeros((SUB, LANES), jnp.float32)
    z = jnp.zeros((SUB, rows_count), jnp.float32)
    for chunk in range(RADIX):
        b = jnp.concatenate(mixed[chunk], 1)
        bh, bl = split_bf16(b)
        if chunk == 0:
            for load in loads[1:]:
                load.wait()
        th, tl = th_ref[chunk], tl_ref[chunk]
        res = lax.dot_general(th, bh, dims, preferred_element_type=jnp.float32)
        res += lax.dot_general(th, bl, dims, preferred_element_type=jnp.float32)
        res += lax.dot_general(tl, bh, dims, preferred_element_type=jnp.float32)
        for e in range(n_devices):
            for g in range(groups):
                sendbuf[pl.ds(((chunk * n_devices + e) * groups + g) * SUB, SUB), :] = (
                    res[e * SUB:(e + 1) * SUB, g * LANES:(g + 1) * LANES])
        if chunk == 0:
            pl.semaphore_wait(barrier, len(peers))
        if chunk < RADIX - 1:
            send(chunk)
        z += jnp.dot(cf_ref[chunk], res, precision=lax.Precision.HIGHEST, preferred_element_type=jnp.float32)
        sq = jnp.sum((res * res).reshape(-1, SUB, rows_count), 0)
        for g in range(groups):
            squares += sq[:, g * LANES:(g + 1) * LANES]
        if chunk == RADIX - 1:
            cosr, sinr, zr, zi = cr_ref[0:1, :], cr_ref[1:2, :], z[0:1, :], z[1:2, :]
            zre, zim = zr * cosr + zi * sinr, zi * cosr - zr * sinr
            fold = lambda v: sum(v[:, g * LANES:(g + 1) * LANES] for g in range(groups))
            stat_out[...] = jnp.concatenate(
                [jnp.sum(squares, 0, keepdims=True), fold(zre), fold(zim),
                 jnp.zeros((SUB - 3, LANES), jnp.float32)], 0)
            stats[pl.ds(slot, 1)] = stat_out[...][None]
            for n in range(len(peers)):
                stat_copy(n).start()
            send(chunk)

    def out_copy(g):
        rows = pl.ds(g * 2 * LANES, 2 * LANES)
        return pltpu.make_async_copy(out_ref.at[rows], out_hbm.at[rows], out_sem.at[g])

    def finish_sums():
        for n in range(len(peers)):
            stat_copy(n).wait_recv()
        t0 = t1 = t2 = jnp.zeros((SUB, LANES), jnp.float32)
        for q in range(n_devices):
            angle = 2.0 * math.pi * q / total_len
            v = stats[q]
            t0, t1, t2 = t0 + v, t1 + v * math.cos(angle), t2 + v * math.sin(angle)
        re = t1[1:2] + t2[2:3]
        im = t1[2:3] - t2[1:2]
        sums = jnp.concatenate([t0[0:1], re, im, jnp.zeros((SUB - 3, LANES), jnp.float32)], 0)
        sums = jnp.sum(sums, 1, keepdims=True)
        mean_square = jnp.broadcast_to(sums[0:1], (SUB, LANES)) / total_len
        shifted = mean_square + 1e-06
        factor = lax.rsqrt(shifted)
        factor = factor * (1.5 - 0.5 * shifted * factor * factor)
        scaled = factor / math.sqrt(total_len)
        lane = lax.broadcasted_iota(jnp.int32, (SUB, LANES), 1)
        fac_ref[...] = factor
        tot_ref[...] = jnp.where(lane == 0, mean_square, jnp.where(lane == 1, sums[1:2], sums[2:3]) * scaled)

    gbits = groups.bit_length() - 1
    for chunk in range(RADIX):
        for n in range(len(peers)):
            data_copy(chunk, n).wait_recv()
        own_copy(chunk).wait()
        for h in range(SUB):
            g = (h // 2) * RADIX + chunk
            tile = jnp.concatenate(
                [recv[pl.ds((chunk * n_devices * groups + rev(j, gbits)) * SUB + h, n_devices, stride=block), :]
                 for j in range(groups)], 0)
            turned = swap_sublanes(tile.T.reshape(LANES // SUB, SUB, LANES))
            for a in range(LANES // SUB):
                out_ref[pl.ds((g * LANES + rev(a, 4)) * 2 + h % 2, SUB, stride=2 * LANES // SUB), :] = turned[a]
            if h % 2:
                out_copy(g).start()
        if chunk == RADIX - 2:
            finish_sums()
    for g in range(RADIX * SUB // 2):
        out_copy(g).wait()
    for n in range(len(peers)):
        stat_copy(n).wait_send()
        for chunk in range(RADIX):
            data_copy(chunk, n).wait_send()


def scale_kernel(field_hbm, tot_ref, fac_ref, out_hbm, checks_ref, field, out, sem):
    size = field.shape[0] // STEPS
    pieces = [pl.ds(k * size, size) for k in range(STEPS)]
    loads = [pltpu.make_async_copy(field_hbm.at[p], field.at[p], sem.at[0, k]) for k, p in enumerate(pieces)]
    stores = [pltpu.make_async_copy(out.at[p], out_hbm.at[p], sem.at[1, k]) for k, p in enumerate(pieces)]
    for load in loads:
        load.start()
    checks_ref[...] = tot_ref[0:1, 0:3]
    for piece, load, store in zip(pieces, loads, stores):
        load.wait()
        out[piece, :] = (field[piece, :].reshape(-1, SUB, LANES) * fac_ref[...][None]).reshape(size, LANES)
        store.start()
    for store in stores:
        store.wait()


def fast(n_outer, n_inner, amplitudes):
    amp_dev = amplitudes.shape[1]
    n_devices = n_outer * n_inner
    rows_count = amp_dev // COLUMNS
    total_len = amp_dev * n_devices
    view = amplitudes.reshape(2, amp_dev // LANES, LANES).transpose(1, 0, 2).reshape(-1, LANES)
    table, cf, cr = tables(rows_count, n_devices)
    th = table.astype(jnp.bfloat16)
    tl = (table - th.astype(np.float32)).astype(jnp.bfloat16)
    vmem = pl.BlockSpec(memory_space=pltpu.VMEM)
    n_peers = n_devices - 1
    field, tot, fac = pl.pallas_call(
        functools.partial(kernel, n_outer, n_inner, rows_count, total_len),
        out_shape=(jax.ShapeDtypeStruct(view.shape, jnp.float32), *[jax.ShapeDtypeStruct((SUB, LANES), jnp.float32)] * 2),
        in_specs=[pl.BlockSpec(memory_space=pltpu.HBM)] * 5,
        out_specs=(pl.BlockSpec(memory_space=pltpu.HBM), vmem, vmem),
        scratch_shapes=[
            pltpu.VMEM(view.shape, jnp.float32),
            pltpu.VMEM(th.shape, jnp.bfloat16),
            pltpu.VMEM(tl.shape, jnp.bfloat16),
            pltpu.VMEM(cf.shape, jnp.float32),
            pltpu.VMEM(cr.shape, jnp.float32),
            pltpu.VMEM(view.shape, jnp.float32),
            pltpu.VMEM(view.shape, jnp.float32),
            pltpu.VMEM(view.shape, jnp.float32),
            pltpu.VMEM((SUB, LANES), jnp.float32),
            pltpu.VMEM((n_devices, SUB, LANES), jnp.float32),
            pltpu.SemaphoreType.DMA((RADIX, n_peers)),
            pltpu.SemaphoreType.DMA((RADIX, n_peers)),
            pltpu.SemaphoreType.DMA((RADIX,)),
            pltpu.SemaphoreType.DMA((n_peers,)),
            pltpu.SemaphoreType.DMA((n_peers,)),
            pltpu.SemaphoreType.DMA((5,)),
            pltpu.SemaphoreType.DMA((RADIX * SUB // 2,)),
        ],
        compiler_params=pltpu.CompilerParams(collective_id=0, has_side_effects=True,
                                             vmem_limit_bytes=63_500_000),
    )(view, jnp.asarray(th), jnp.asarray(tl), jnp.asarray(cf), jnp.asarray(cr))
    hbm = pl.BlockSpec(memory_space=pltpu.HBM)
    field, checks = pl.pallas_call(
        scale_kernel,
        out_shape=(jax.ShapeDtypeStruct(view.shape, jnp.float32), jax.ShapeDtypeStruct((1, 3), jnp.float32)),
        in_specs=[hbm, vmem, vmem],
        out_specs=(hbm, vmem),
        scratch_shapes=[
            pltpu.VMEM(view.shape, jnp.float32),
            pltpu.VMEM(view.shape, jnp.float32),
            pltpu.SemaphoreType.DMA((2, STEPS)),
        ],
        compiler_params=pltpu.CompilerParams(vmem_limit_bytes=63_500_000),
    )(field, tot, fac)
    result = field.reshape(-1, 2, LANES).transpose(1, 0, 2).reshape(2, amp_dev)
    return result, checks.reshape(3)


def reverse_index(values, count):
    result = jnp.zeros_like(values)
    for bit_pos in range(count):
        result = result | (values >> bit_pos & 1) << count - 1 - bit_pos
    return result


def reversal_table(size, count):
    indices = jnp.arange(size, dtype=jnp.int32)
    return (reverse_index(indices, count)[:, None] == indices[None, :]).astype(jnp.float32)


def check_terms(current, positions, angle_scale):
    angles = positions.astype(jnp.float32) * angle_scale
    cosine = jnp.cos(angles)
    sine = jnp.sin(angles)
    squares = jnp.sum(current * current)
    phase_real = jnp.sum(current[0] * cosine + current[1] * sine)
    phase_imag = jnp.sum(current[1] * cosine - current[0] * sine)
    return (squares, phase_real, phase_imag)


def per_device(amplitudes):
    amp_dev = amplitudes.shape[1]
    n_outer = lax.axis_size("outer")
    n_inner = lax.axis_size("inner")
    outer_bits = n_outer.bit_length() - 1
    inner_bits = n_inner.bit_length() - 1
    global_bits = outer_bits + inner_bits
    local_bits = amp_dev.bit_length() - 1
    n_devices = n_outer * n_inner
    high_count = amp_dev // n_devices
    total_len = amp_dev * n_devices
    columns = 2**WINDOW
    rows_count = amp_dev // columns
    column_ids = jnp.arange(columns, dtype=jnp.int32)
    reversed_ids = reverse_index(column_ids, WINDOW)
    products = column_ids[:, None] * reversed_ids[None, :] % columns
    angles = products.astype(jnp.float32) * (2.0 * math.pi / columns)
    real_part = jnp.cos(angles) / math.sqrt(columns)
    imag_part = jnp.sin(angles) / math.sqrt(columns)
    table = jnp.concatenate(
        [jnp.concatenate([real_part, imag_part], 1), jnp.concatenate([-imag_part, real_part], 1)], 0
    )
    stacked = jnp.concatenate(
        [amplitudes[0].reshape(rows_count, columns), amplitudes[1].reshape(rows_count, columns)], 1
    )
    result = jnp.dot(
        stacked, table, precision=lax.Precision.HIGHEST, preferred_element_type=jnp.float32
    )
    windowed = jnp.stack([result[:, :columns].reshape(-1), result[:, columns:].reshape(-1)])
    device_id = lax.axis_index("outer") * n_inner + lax.axis_index("inner")
    angle_scale = 2.0 * math.pi / total_len
    local_ids = jnp.arange(amp_dev, dtype=jnp.int32)
    positions = reverse_index(device_id * amp_dev + local_ids, local_bits + global_bits)
    totals = lax.psum(check_terms(windowed, positions, angle_scale), ("outer", "inner"))
    device_table = reversal_table(n_devices, global_bits)
    high_table = reversal_table(high_count, local_bits - global_bits)
    grid = windowed.reshape(2, high_count, n_devices)
    ordered = jnp.einsum("pm,shm->sph", device_table, grid, precision=lax.Precision.HIGHEST)
    blocks = ordered.reshape(2, n_outer, n_inner, high_count)
    blocks = lax.all_to_all(
        lax.all_to_all(blocks, "outer", split_axis=1, concat_axis=1, tiled=True),
        "inner",
        split_axis=2,
        concat_axis=2,
        tiled=True,
    )
    received = blocks.reshape(2, n_devices, high_count)
    turned_high = jnp.einsum("qh,sdh->sdq", high_table, received, precision=lax.Precision.HIGHEST)
    placed = jnp.einsum("ed,sdq->sqe", device_table, turned_high, precision=lax.Precision.HIGHEST)
    reversed_field = placed.reshape(2, amp_dev)
    mean_square = totals[0] / total_len
    factor = lax.rsqrt(mean_square + 1e-06)
    scaled = factor / math.sqrt(total_len)
    checks = jnp.stack([mean_square, totals[1] * scaled, totals[2] * scaled])
    return (reversed_field * factor, checks)


def solution(mesh):
    n_outer, n_inner = mesh.shape["outer"], mesh.shape["inner"]

    def body(amplitudes):
        rows_count = amplitudes.shape[1] // COLUMNS
        n_devices = n_outer * n_inner
        if rows_count * n_devices == LANES * LANES and n_devices * SUB == 2 * LANES:
            return fast(n_outer, n_inner, amplitudes)
        return per_device(amplitudes)

    return jax.shard_map(
        body,
        mesh=mesh,
        in_specs=(P(None, ("outer", "inner")),),
        out_specs=(P(None, ("outer", "inner")), P()),
        check_vma=False,
    )
```

profile of v0, /device:TPU:0, one launch (start us, length us, event | category | flops | bytes accessed | tf_op | source)
XLA Modules:
  0.0 64.8 jit_solution(3339069071101458703)
XLA Ops:
  0.6 60.5 %shard_map.68 = (f32[4096,128]{1,0:T(8,128)}, f32[8,128]{1,0:T(8,128)}, f32[8,128]{1,0:T(8,128)}) custom-call(f32[4096,128]{1,0:T(8,128)} %bitcast.11, bf16[4,256,256]{2,1,0:T(8,128)(2,1)} %constant.8.clone.th_hbm, bf16[4,256,256]{2,1,0:T(8,128)(2,1)} %constant.9.clone.tl_hbm, f32[4,8,256]{2,1,0:T(8,128)} %constant.10.clone.cf_hbm, ...), custom_call_target="tpu_custom_call" | custom-call | tf_op jit(solution)/shard_map/pallas_call | solution.py:247
  61.2 3.6 %shard_map.69 = (f32[4096,128]{1,0:T(8,128)}, f32[1,3]{1,0:T(1,128)}) custom-call(f32[4096,128]{1,0:T(8,128)} %get-tuple-element.7.field_hbm, f32[8,128]{1,0:T(8,128)} %get-tuple-element.8.tot_ref, f32[8,128]{1,0:T(8,128)} %get-tuple-element.9.fac_ref), custom_call_target="tpu_custom_call" | custom-call | tf_op jit(solution)/shard_map/pallas_call | solution.py:275
where the time goes:
time: 65 us; the launch traced here: 64.8 us
  Pallas kernels  64.2 us (99%)
    pallas_call x1, Pallas kernels, fast(): pl.pallas_call(functools.partial(kernel, n_outer, n_inner, rows_count, to...  60.5 us
    pallas_call x1, Pallas kernels, fast(): pl.pallas_call(scale_kernel, out_shape=(jax.ShapeDtypeStruct(view.shape,...  3.61 us

commit v1 on v0

v1 whole, which is shorter than its diff:
```python
import functools
import math

import jax
import jax.numpy as jnp
import numpy as np
from jax import lax
from jax.experimental import pallas as pl
from jax.experimental.pallas import tpu as pltpu
from jax.sharding import PartitionSpec as P

WINDOW = 9
COLUMNS = 2**WINDOW
LANES = 128
SUB = 8
RADIX = COLUMNS // LANES
PIECES = ((0,), (1, 2), (3,))
MESH = pl.DeviceIdType.MESH


def rev(value, count):
    out = 0
    for bit in range(count):
        out |= (value >> bit & 1) << (count - 1 - bit)
    return out


def split_bf16(values):
    high = values.astype(jnp.bfloat16)
    return high, (values - high.astype(np.float32)).astype(jnp.bfloat16)


def tables(n_devices, total_len):
    f = np.arange(COLUMNS).reshape(LANES, RADIX).T
    lane = np.arange(LANES)
    ang = (f[:, :, None] * lane) % COLUMNS * (2.0 * np.pi / COLUMNS)
    c, s = np.cos(ang) / math.sqrt(COLUMNS), np.sin(ang) / math.sqrt(COLUMNS)
    table = np.stack([np.concatenate([c, -s], -1), np.concatenate([s, c], -1)], 2)
    table = table.reshape(RADIX, 2 * LANES, 2 * LANES).astype(np.float32)
    slots = 2.0 * np.pi / total_len * np.arange(n_devices)
    subs = 2.0 * np.pi / total_len * n_devices * RADIX * np.arange(SUB)
    turn = np.zeros((2 * (n_devices + SUB), LANES), np.float32)
    turn[:n_devices], turn[n_devices : 2 * n_devices] = np.cos(slots)[:, None], np.sin(slots)[:, None]
    turn[2 * n_devices : 2 * n_devices + SUB, 1] = np.cos(subs) * math.sqrt(COLUMNS)
    turn[2 * n_devices + SUB :, 1] = np.sin(subs) * math.sqrt(COLUMNS)
    return table, turn


def pieces_of(n_devices):
    rows = [len(chunks) * RADIX * SUB + (k == 0) for k, chunks in enumerate(PIECES)]
    return rows, [r if r % 2 else r + 4 for r in rows]


def turn_tiles(recv, pitch, place, h, n_devices, factor):
    tile = jnp.concatenate(
        [recv[pl.ds((place * RADIX + rev(j, 2)) * SUB + h, n_devices, stride=pitch), :] for j in range(RADIX)], 0)
    turned = tile.T.reshape(LANES // SUB, SUB, LANES)
    return [turned[m] * factor for m in range(LANES // SUB)]


def kernel(n_outer, n_inner, total_len, x_hbm, th_hbm, tl_hbm, turn_hbm, *refs):
    n_pieces = len(PIECES)
    field, last, tot_ref, fac_ref, x_ref, th_ref, tl_ref, turn_ref, bh_ref, bl_ref = refs[:10]
    sends, recvs = refs[10 : 10 + n_pieces], [*refs[10 + n_pieces : 9 + 2 * n_pieces], last]
    send_sem, recv_sem, own_sem, load_sem = refs[9 + 2 * n_pieces :]
    n_devices = n_outer * n_inner
    obits, ibits = n_outer.bit_length() - 1, n_inner.bit_length() - 1
    span = LANES
    q_rows = span + 4

    loads = []
    for g in range(RADIX):
        for q in range(SUB):
            loads.append(pltpu.make_async_copy(
                x_hbm.at[pl.ds((g * SUB + q) * span, span)],
                x_ref.at[pl.ds((g * SUB + rev(q, 3)) * q_rows, span)], load_sem.at[g]))
    rest = [pltpu.make_async_copy(src, dst, load_sem.at[RADIX + k]) for k, (src, dst) in enumerate(
        [(th_hbm, th_ref), (tl_hbm, tl_ref), (turn_hbm, turn_ref)])]
    for load in loads + rest:
        load.start()

    o, i = lax.axis_index("outer"), lax.axis_index("inner")
    me = o * n_inner + i
    slot = 0
    odelta, idelta = [], []
    for k in range(obits):
        bit = o // 2**k % 2
        slot = slot + bit * 2 ** (obits - 1 - k)
        odelta.append((1 - 2 * bit) * 2**k)
    for k in range(ibits):
        bit = i // 2**k % 2
        slot = slot + bit * 2 ** (ibits - 1 - k) * n_outer
        idelta.append((1 - 2 * bit) * 2**k)

    def peer(mo, mi):
        po, pi = o, i
        for k in range(obits):
            if mo >> k & 1:
                po = po + odelta[k]
        for k in range(ibits):
            if mi >> k & 1:
                pi = pi + idelta[k]
        return po, pi

    peers = [peer(mo, mi) for mi in range(n_inner - 1, -1, -1) for mo in range(n_outer) if mo or mi]
    barrier = pltpu.get_barrier_semaphore()
    for p in peers:
        pl.semaphore_signal(barrier, inc=1, device_id=p, device_id_type=MESH)

    rows, pitches = pieces_of(n_devices)

    def send(k):
        dst = recvs[k].at[pl.ds(slot * pitches[k], rows[k])]
        for po, pi in peers:
            pltpu.make_async_remote_copy(
                src_ref=sends[k].at[pl.ds((po * n_inner + pi) * rows[k], rows[k])], dst_ref=dst,
                send_sem=send_sem, recv_sem=recv_sem.at[k],
                device_id=(po, pi), device_id_type=MESH).start()
        own_copy(k).start()

    def own_copy(k):
        return pltpu.make_async_copy(
            sends[k].at[pl.ds(me * rows[k], rows[k])],
            recvs[k].at[pl.ds(slot * pitches[k], rows[k])], own_sem.at[k])

    def wait_rows(ref, count, sem):
        part = ref.at[pl.ds(0, count)]
        pltpu.make_async_copy(part, part, sem).wait()

    zero = jnp.zeros((SUB, LANES), jnp.float32)
    squares, zr, zi = [zero] * 4, zero, zero
    for g in range(RADIX):
        wait_rows(x_ref, SUB * span, load_sem.at[g])
        for pair in range(SUB):
            part = [[[x_ref[pl.ds(g * SUB * q_rows + (2 * pair + w) * SUB + 2 * ct + s, SUB, stride=q_rows), :]
                      for w in range(2)] for s in range(2)] for ct in range(RADIX)]
            for ct in range(RADIX):
                for s in range(2):
                    for w in range(2):
                        squares[ct] = squares[ct] + part[ct][s][w] * part[ct][s][w]
            for w in range(2):
                angle = 2.0 * math.pi / total_len * n_devices * (rev(2 * pair + w, 4) * SUB * RADIX + rev(g, 2))
                cw, sw = math.cos(angle), math.sin(angle)
                zr = zr + (part[0][0][w] * cw + part[0][1][w] * sw)
                zi = zi + (part[0][1][w] * cw - part[0][0][w] * sw)
            (x0r, x0i), (x1r, x1i), (x2r, x2i), (x3r, x3i) = [
                [jnp.concatenate(part[ct][s], 0) for s in range(2)] for ct in range(RADIX)]
            ar, ai, br, bi = x0r + x2r, x0i + x2i, x0r - x2r, x0i - x2i
            cr_, ci_, dr, di = x1r + x3r, x1i + x3i, x1r - x3r, x1i - x3i
            mixed = [(ar + cr_, ai + ci_), (br - di, bi + dr), (ar - cr_, ai - ci_), (br + di, bi - dr)]
            at = pl.ds((g * SUB + pair) * 2 * SUB, 2 * SUB)
            for chunk in range(RADIX):
                for s in range(2):
                    high, low = split_bf16(mixed[chunk][s])
                    bh_ref[chunk, at, s * LANES : (s + 1) * LANES] = high
                    bl_ref[chunk, at, s * LANES : (s + 1) * LANES] = low

    for load in rest:
        load.wait()
    pc, ps = turn_ref[2 * n_devices : 2 * n_devices + SUB, :], turn_ref[2 * n_devices + SUB :, :]
    oc, os_ = turn_ref[pl.ds(slot, 1), :], turn_ref[pl.ds(n_devices + slot, 1), :]
    total = jnp.sum(jnp.sum((squares[0] + squares[1]) + (squares[2] + squares[3]), 0, keepdims=True), 1, keepdims=True)
    yr = jnp.sum(zr * pc + zi * ps, 0, keepdims=True)
    yi = jnp.sum(zi * pc - zr * ps, 0, keepdims=True)
    wr = jnp.sum(yr * oc + yi * os_, 1, keepdims=True)
    wi = jnp.sum(yi * oc - yr * os_, 1, keepdims=True)
    lane = lax.broadcasted_iota(jnp.int32, (1, LANES), 1)
    stat = jnp.where(lane == 0, total, jnp.where(lane == 1, wr, jnp.where(lane == 2, wi, 0.0)))
    sends[0][pl.ds(rows[0] - 1, n_devices, stride=rows[0]), :] = jnp.broadcast_to(stat, (n_devices, LANES))

    dims = (((1,), (1,)), ((), ()))
    for k, chunks in enumerate(PIECES):
        for place, chunk in enumerate(chunks):
            th, tl, bh, bl = th_ref[chunk], tl_ref[chunk], bh_ref[chunk], bl_ref[chunk]
            res = lax.dot_general(th, bh, dims, preferred_element_type=jnp.float32)
            res += lax.dot_general(th, bl, dims, preferred_element_type=jnp.float32)
            res += lax.dot_general(tl, bh, dims, preferred_element_type=jnp.float32)
            for e in range(n_devices):
                for g in range(RADIX):
                    sends[k][pl.ds(e * rows[k] + (place * RADIX + g) * SUB, SUB), :] = (
                        res[e * SUB : (e + 1) * SUB, g * LANES : (g + 1) * LANES])
        if k == 0:
            pl.semaphore_wait(barrier, len(peers))
        send(k)

    for k, chunks in enumerate(PIECES):
        wait_rows(recvs[k], len(peers) * rows[k], recv_sem.at[k])
        own_copy(k).wait()
        if k == 0:
            sums = jnp.sum(recvs[0][pl.ds(rows[0] - 1, n_devices, stride=pitches[0]), :], 0, keepdims=True)
            mean_square = jnp.sum(jnp.where(lane == 0, sums, 0.0), 1, keepdims=True) / total_len
            shifted = mean_square + 1e-06
            factor = lax.rsqrt(shifted)
            factor = factor * (1.5 - 0.5 * shifted * factor * factor)
            checks = jnp.where(lane == 0, mean_square, sums * (factor / math.sqrt(total_len)))
            tot_ref[...] = jnp.broadcast_to(checks, (SUB, LANES))
            factor = jnp.broadcast_to(factor, (SUB, LANES))
            fac_ref[...] = factor
        if k == n_pieces - 1:
            break
        for place, chunk in enumerate(chunks):
            for h in range(SUB):
                base = ((h // 2) * (RADIX - 1) + chunk) * 2 * LANES + h % 2
                for m, v in enumerate(turn_tiles(recvs[k], pitches[k], place, h, n_devices, factor)):
                    field[pl.ds(base + rev(m, 4) * 2 * SUB, SUB, stride=2), :] = v
    for k in range(n_pieces):
        wait_rows(sends[k], len(peers) * rows[k], send_sem)


def finish_kernel(n_devices, pitch, field, last, tot_ref, fac_ref, out_hbm, checks_ref, turned, sem):
    f_rows = 2 * LANES
    many = (RADIX - 1) * f_rows
    stores = []
    for fq in range(RADIX):
        stores.append(pltpu.make_async_copy(
            field.at[pl.ds(fq * many, many)], out_hbm.at[pl.ds(fq * RADIX * f_rows, many)], sem.at[fq]))
        stores[-1].start()
    checks_ref[...] = tot_ref[0:1, 0:3]
    factor = fac_ref[...]
    for h in range(SUB):
        base = h // 2 * f_rows + h % 2
        for m, v in enumerate(turn_tiles(last, pitch, 0, h, n_devices, factor)):
            turned[pl.ds(base + rev(m, 4) * 2 * SUB, SUB, stride=2), :] = v
        if h % 2:
            fq = h // 2
            stores.append(pltpu.make_async_copy(
                turned.at[pl.ds(fq * f_rows, f_rows)],
                out_hbm.at[pl.ds((fq * RADIX + RADIX - 1) * f_rows, f_rows)], sem.at[RADIX + fq]))
            stores[-1].start()
    for store in stores:
        store.wait()


def fast(n_outer, n_inner, amplitudes):
    amp_dev = amplitudes.shape[1]
    n_devices = n_outer * n_inner
    rows_count = amp_dev // COLUMNS
    total_len = amp_dev * n_devices
    view = amplitudes.reshape(2, amp_dev // LANES, LANES).transpose(1, 0, 2).reshape(-1, LANES)
    table, turn = tables(n_devices, total_len)
    th = table.astype(jnp.bfloat16)
    tl = (table - th.astype(np.float32)).astype(jnp.bfloat16)
    hbm, vmem = pl.BlockSpec(memory_space=pltpu.HBM), pl.BlockSpec(memory_space=pltpu.VMEM)
    rows, pitches = pieces_of(n_devices)
    small = pltpu.VMEM((SUB, LANES), jnp.float32)
    f_rows = 2 * LANES
    pair = pltpu.VMEM((RADIX, rows_count, 2 * LANES), jnp.bfloat16)
    scratch = [
        pltpu.VMEM((RADIX * SUB * (LANES + 4), LANES), jnp.float32),
        pltpu.VMEM(th.shape, jnp.bfloat16),
        pltpu.VMEM(tl.shape, jnp.bfloat16),
        pltpu.VMEM(turn.shape, jnp.float32),
        pair,
        pair,
        *[pltpu.VMEM((n_devices * r, LANES), jnp.float32) for r in rows],
        *[pltpu.VMEM((n_devices * p, LANES), jnp.float32) for p in pitches[:-1]],
        pltpu.SemaphoreType.DMA,
        pltpu.SemaphoreType.DMA((len(PIECES),)),
        pltpu.SemaphoreType.DMA((len(PIECES),)),
        pltpu.SemaphoreType.DMA((RADIX + 3,)),
    ]
    parts = pl.pallas_call(
        functools.partial(kernel, n_outer, n_inner, total_len),
        out_shape=(
            pltpu.VMEM((RADIX * (RADIX - 1) * f_rows, LANES), jnp.float32),
            pltpu.VMEM((n_devices * pitches[-1], LANES), jnp.float32),
            small,
            small,
        ),
        in_specs=[hbm] * 4,
        out_specs=(vmem,) * 4,
        scratch_shapes=scratch,
        compiler_params=pltpu.CompilerParams(collective_id=0, has_side_effects=True, vmem_limit_bytes=32_000_000),
    )(view, jnp.asarray(th), jnp.asarray(tl), jnp.asarray(turn))
    field, checks = pl.pallas_call(
        functools.partial(finish_kernel, n_devices, pitches[-1]),
        out_shape=(jax.ShapeDtypeStruct(view.shape, jnp.float32), jax.ShapeDtypeStruct((1, 3), jnp.float32)),
        in_specs=[vmem] * 4,
        out_specs=(hbm, vmem),
        scratch_shapes=[
            pltpu.VMEM((RADIX * f_rows, LANES), jnp.float32),
            pltpu.SemaphoreType.DMA((2 * RADIX,)),
        ],
        compiler_params=pltpu.CompilerParams(vmem_limit_bytes=32_000_000),
    )(*parts)
    result = field.reshape(-1, 2, LANES).transpose(1, 0, 2).reshape(2, amp_dev)
    return result, checks.reshape(3)


def reverse_index(values, count):
    result = jnp.zeros_like(values)
    for bit_pos in range(count):
        result = result | (values >> bit_pos & 1) << count - 1 - bit_pos
    return result


def reversal_table(size, count):
    indices = jnp.arange(size, dtype=jnp.int32)
    return (reverse_index(indices, count)[:, None] == indices[None, :]).astype(jnp.float32)


def check_terms(current, positions, angle_scale):
    angles = positions.astype(jnp.float32) * angle_scale
    cosine = jnp.cos(angles)
    sine = jnp.sin(angles)
    squares = jnp.sum(current * current)
    phase_real = jnp.sum(current[0] * cosine + current[1] * sine)
    phase_imag = jnp.sum(current[1] * cosine - current[0] * sine)
    return (squares, phase_real, phase_imag)


def per_device(amplitudes):
    amp_dev = amplitudes.shape[1]
    n_outer = lax.axis_size("outer")
    n_inner = lax.axis_size("inner")
    outer_bits = n_outer.bit_length() - 1
    inner_bits = n_inner.bit_length() - 1
    global_bits = outer_bits + inner_bits
    local_bits = amp_dev.bit_length() - 1
    n_devices = n_outer * n_inner
    high_count = amp_dev // n_devices
    total_len = amp_dev * n_devices
    columns = 2**WINDOW
    rows_count = amp_dev // columns
    column_ids = jnp.arange(columns, dtype=jnp.int32)
    reversed_ids = reverse_index(column_ids, WINDOW)
    products = column_ids[:, None] * reversed_ids[None, :] % columns
    angles = products.astype(jnp.float32) * (2.0 * math.pi / columns)
    real_part = jnp.cos(angles) / math.sqrt(columns)
    imag_part = jnp.sin(angles) / math.sqrt(columns)
    table = jnp.concatenate(
        [jnp.concatenate([real_part, imag_part], 1), jnp.concatenate([-imag_part, real_part], 1)], 0
    )
    stacked = jnp.concatenate(
        [amplitudes[0].reshape(rows_count, columns), amplitudes[1].reshape(rows_count, columns)], 1
    )
    result = jnp.dot(
        stacked, table, precision=lax.Precision.HIGHEST, preferred_element_type=jnp.float32
    )
    windowed = jnp.stack([result[:, :columns].reshape(-1), result[:, columns:].reshape(-1)])
    device_id = lax.axis_index("outer") * n_inner + lax.axis_index("inner")
    angle_scale = 2.0 * math.pi / total_len
    local_ids = jnp.arange(amp_dev, dtype=jnp.int32)
    positions = reverse_index(device_id * amp_dev + local_ids, local_bits + global_bits)
    totals = lax.psum(check_terms(windowed, positions, angle_scale), ("outer", "inner"))
    device_table = reversal_table(n_devices, global_bits)
    high_table = reversal_table(high_count, local_bits - global_bits)
    grid = windowed.reshape(2, high_count, n_devices)
    ordered = jnp.einsum("pm,shm->sph", device_table, grid, precision=lax.Precision.HIGHEST)
    blocks = ordered.reshape(2, n_outer, n_inner, high_count)
    blocks = lax.all_to_all(
        lax.all_to_all(blocks, "outer", split_axis=1, concat_axis=1, tiled=True),
        "inner",
        split_axis=2,
        concat_axis=2,
        tiled=True,
    )
    received = blocks.reshape(2, n_devices, high_count)
    turned_high = jnp.einsum("qh,sdh->sdq", high_table, received, precision=lax.Precision.HIGHEST)
    placed = jnp.einsum("ed,sdq->sqe", device_table, turned_high, precision=lax.Precision.HIGHEST)
    reversed_field = placed.reshape(2, amp_dev)
    mean_square = totals[0] / total_len
    factor = lax.rsqrt(mean_square + 1e-06)
    scaled = factor / math.sqrt(total_len)
    checks = jnp.stack([mean_square, totals[1] * scaled, totals[2] * scaled])
    return (reversed_field * factor, checks)


def solution(mesh):
    n_outer, n_inner = mesh.shape["outer"], mesh.shape["inner"]

    def body(amplitudes):
        rows_count = amplitudes.shape[1] // COLUMNS
        n_devices = n_outer * n_inner
        if rows_count * n_devices == LANES * LANES and n_devices * SUB == 2 * LANES:
            return fast(n_outer, n_inner, amplitudes)
        return per_device(amplitudes)

    return jax.shard_map(
        body,
        mesh=mesh,
        in_specs=(P(None, ("outer", "inner")),),
        out_specs=(P(None, ("outer", "inner")), P()),
        check_vma=False,
    )
```

time: 65 us -> 64.5 us (level)
  Pallas kernels: 64.2 us -> 59.1 us
  local copies, waits for them, and re-layouts: 0 us -> 4.44 us
    pallas_call x2, Pallas kernels: 64.2 us -> 59.1 us  [the longest x1 57.2 us: fast(): pl.pallas_call(functools.partial(kernel, n_outer, n_inner, total_len), ou...]
    unnamed x0 -> x8, local copies, waits for them, and re-layouts: none -> 4.44 us
where the time goes in v1:
time: 64.5 us; the launch traced here: 64.2 us
  Pallas kernels  59.1 us (92%)
  local copies, waits for them, and re-layouts  4.44 us (7%)
  between operations  0.65 us (1%)
    pallas_call x1, Pallas kernels, fast(): pl.pallas_call(functools.partial(kernel, n_outer, n_inner, total_len), ou...  57.2 us
    unnamed x8, local copies, waits for them, and re-layouts  4.44 us
    pallas_call x1, Pallas kernels, fast(): pl.pallas_call(functools.partial(finish_kernel, n_devices, pitches[-1]),...  1.9 us

profile of v1, /device:TPU:0, one launch (start us, length us, event | category | flops | bytes accessed | tf_op | source)
XLA Modules:
  0.0 64.2 jit_solution(10197686669771978462)
XLA Ops:
  0.6 0.0 copy-start
  0.6 1.6 %copy-done = f32[2,262144]{1,0:T(2,128)S(1)} copy-done((f32[2,262144]{1,0:T(2,128)S(1)}, f32[2,262144]{1,0:T(2,128)}, u32[]{:S(2)}) %copy-start) | copy-done | bytes 2097176
  2.2 0.0 copy-start.1
  2.2 1.0 %copy-done.1 = bf16[4,256,256]{2,1,0:T(8,128)(2,1)S(1)} copy-done((bf16[4,256,256]{2,1,0:T(8,128)(2,1)S(1)}, bf16[4,256,256]{2,1,0:T(8,128)(2,1)}, u32[]{:S(2)}) %copy-start.1) | copy-done | bytes 524312
  3.3 0.0 copy-start.2
  3.3 1.0 %copy-done.2 = bf16[4,256,256]{2,1,0:T(8,128)(2,1)S(1)} copy-done((bf16[4,256,256]{2,1,0:T(8,128)(2,1)S(1)}, bf16[4,256,256]{2,1,0:T(8,128)(2,1)}, u32[]{:S(2)}) %copy-start.2) | copy-done | bytes 524312
  4.3 0.0 copy-start.3
  4.3 0.8 %copy-done.3 = f32[80,128]{1,0:T(8,128)S(1)} copy-done((f32[80,128]{1,0:T(8,128)S(1)}, f32[80,128]{1,0:T(8,128)}, u32[]{:S(2)}) %copy-start.3) | copy-done | bytes 40984
  5.1 57.2 %shard_map.59 = (f32[3072,128]{1,0:T(8,128)S(1)}, f32[1152,128]{1,0:T(8,128)S(1)}, f32[8,128]{1,0:T(8,128)S(1)}, f32[8,128]{1,0:T(8,128)S(1)}) custom-call(f32[4096,128]{1,0:T(8,128)S(1)} %bitcast.11, bf16[4,256,256]{2,1,0:T(8,128)(2,1)S(1)} %copy-done.2, bf16[4,256,256]{2,1,0:T(8,128)(2,1)S(1)} %copy-done.1, f32[80,128]{1,0:T(8,128)S(1)} %copy-done.3), custom_call_target="tpu_custom_call" | custom-call | tf_op jit(solution)/shard_map/pallas_call | solution.py:262
  62.3 1.9 %shard_map.60 = (f32[4096,128]{1,0:T(8,128)}, f32[1,3]{1,0:T(1,128)}) custom-call(f32[3072,128]{1,0:T(8,128)S(1)} %get-tuple-element.8.field, f32[1152,128]{1,0:T(8,128)S(1)} %get-tuple-element.9.last, f32[8,128]{1,0:T(8,128)S(1)} %get-tuple-element.10.tot_ref, f32[8,128]{1,0:T(8,128)S(1)} %get-tuple-element.11.fac_ref), custom_call_target="tpu_custom_call" | custom-call | tf_op jit(solution)/shard_map/pallas_call | solution.py:275
Async XLA Ops:
  0.6 1.6 %copy-start = (f32[2,262144]{1,0:T(2,128)S(1)}, f32[2,262144]{1,0:T(2,128)}, u32[]{:S(2)}) copy-start(f32[2,262144]{1,0:T(2,128)} %param.4) | copy-start | bytes 6291460
  2.2 1.0 %copy-start.1 = (bf16[4,256,256]{2,1,0:T(8,128)(2,1)S(1)}, bf16[4,256,256]{2,1,0:T(8,128)(2,1)}, u32[]{:S(2)}) copy-start(bf16[4,256,256]{2,1,0:T(8,128)(2,1)} %constant.7.clone.tl_hbm) | copy-start | bytes 1572868
  3.3 1.0 %copy-start.2 = (bf16[4,256,256]{2,1,0:T(8,128)(2,1)S(1)}, bf16[4,256,256]{2,1,0:T(8,128)(2,1)}, u32[]{:S(2)}) copy-start(bf16[4,256,256]{2,1,0:T(8,128)(2,1)} %constant.6.clone.th_hbm) | copy-start | bytes 1572868
  4.3 0.8 %copy-start.3 = (f32[80,128]{1,0:T(8,128)S(1)}, f32[80,128]{1,0:T(8,128)}, u32[]{:S(2)}) copy-start(f32[80,128]{1,0:T(8,128)} %constant.8.clone.turn_hbm) | copy-start | bytes 122884

commit v2 on v1

--- a/solution.py
+++ b/solution.py
@@ -271,7 +271,7 @@
         out_specs=(vmem,) * 4,
         scratch_shapes=scratch,
         compiler_params=pltpu.CompilerParams(collective_id=0, has_side_effects=True, vmem_limit_bytes=32_000_000),
-    )(view, jnp.asarray(th), jnp.asarray(tl), jnp.asarray(turn))
+    )(*[pltpu.with_memory_space_constraint(v, pltpu.HBM) for v in (view, jnp.asarray(th), jnp.asarray(tl), jnp.asarray(turn))])
     field, checks = pl.pallas_call(
         functools.partial(finish_kernel, n_devices, pitches[-1]),
         out_shape=(jax.ShapeDtypeStruct(view.shape, jnp.float32), jax.ShapeDtypeStruct((1, 3), jnp.float32)),

time: 64.5 us -> 57.1 us (0.89)
  local copies, waits for them, and re-layouts: 4.44 us -> 0 us
  Pallas kernels: 59.1 us -> 56.4 us
    unnamed x8 -> x0, local copies, waits for them, and re-layouts: 4.44 us -> none
    pallas_call x1, Pallas kernels: 57.2 us -> 54.5 us  [fast(): pl.pallas_call(functools.partial(kernel, n_outer, n_inner, total_len), ou...]
where the time goes in v2:
time: 57.1 us; the launch traced here: 57 us
  Pallas kernels  56.4 us (99%)
  between operations  0.64 us (1%)
    pallas_call x1, Pallas kernels, fast(): pl.pallas_call(functools.partial(kernel, n_outer, n_inner, total_len), ou...  54.5 us
    pallas_call x1, Pallas kernels, fast(): pl.pallas_call(functools.partial(finish_kernel, n_devices, pitches[-1]),...  1.9 us

profile of v2, /device:TPU:0, one launch (start us, length us, event | category | flops | bytes accessed | tf_op | source)
XLA Modules:
  0.0 57.0 jit_solution(1317455610250523024)
XLA Ops:
  0.6 54.5 %shard_map.59 = (f32[3072,128]{1,0:T(8,128)S(1)}, f32[1152,128]{1,0:T(8,128)S(1)}, f32[8,128]{1,0:T(8,128)S(1)}, f32[8,128]{1,0:T(8,128)S(1)}) custom-call(f32[4096,128]{1,0:T(8,128)} %bitcast.11, bf16[4,256,256]{2,1,0:T(8,128)(2,1)} %constant.6.clone.th_hbm, bf16[4,256,256]{2,1,0:T(8,128)(2,1)} %constant.7.clone.tl_hbm, f32[80,128]{1,0:T(8,128)} %constant.8.clone.turn_hbm), custom_call_target="tpu_custom_call" | custom-call | tf_op jit(solution)/shard_map/pallas_call | solution.py:262
  55.1 1.9 %shard_map.60 = (f32[4096,128]{1,0:T(8,128)}, f32[1,3]{1,0:T(1,128)}) custom-call(f32[3072,128]{1,0:T(8,128)S(1)} %get-tuple-element.8.field, f32[1152,128]{1,0:T(8,128)S(1)} %get-tuple-element.9.last, f32[8,128]{1,0:T(8,128)S(1)} %get-tuple-element.10.tot_ref, f32[8,128]{1,0:T(8,128)S(1)} %get-tuple-element.11.fac_ref), custom_call_target="tpu_custom_call" | custom-call | tf_op jit(solution)/shard_map/pallas_call | solution.py:275

commit v3 on v2

--- a/solution.py
+++ b/solution.py
@@ -1,4 +1,5 @@
 import functools
+import itertools
 import math
 
 import jax
@@ -15,6 +16,7 @@
 SUB = 8
 RADIX = COLUMNS // LANES
 PIECES = ((0,), (1, 2), (3,))
+STAT = 1
 MESH = pl.DeviceIdType.MESH
 
 
@@ -47,7 +49,7 @@
 
 
 def pieces_of(n_devices):
-    rows = [len(chunks) * RADIX * SUB + (k == 0) for k, chunks in enumerate(PIECES)]
+    rows = [len(chunks) * RADIX * SUB + (k == STAT) for k, chunks in enumerate(PIECES)]
     return rows, [r if r % 2 else r + 4 for r in rows]
 
 
@@ -102,7 +104,14 @@
                 pi = pi + idelta[k]
         return po, pi
 
-    peers = [peer(mo, mi) for mi in range(n_inner - 1, -1, -1) for mo in range(n_outer) if mo or mi]
+    half = n_inner // 2
+    high = i // half
+    far = []
+    for t in range(half):
+        pi = high * t + (1 - high) * (n_inner - 1 - t)
+        far += [(peer(mo, 0)[0], pi) for mo in range(n_outer)]
+    near = [peer(mo, mi) for mi in range(half - 1, -1, -1) for mo in range(n_outer) if mo or mi]
+    peers = [p for pair in itertools.zip_longest(far, near) for p in pair if p is not None]
     barrier = pltpu.get_barrier_semaphore()
     for p in peers:
         pl.semaphore_signal(barrier, inc=1, device_id=p, device_id_type=MESH)
@@ -127,13 +136,48 @@
         part = ref.at[pl.ds(0, count)]
         pltpu.make_async_copy(part, part, sem).wait()
 
+    def rows_of(g, pair, ct, s):
+        return [x_ref[pl.ds(g * SUB * q_rows + (2 * pair + w) * SUB + 2 * ct + s, SUB, stride=q_rows), :] for w in range(2)]
+
+    def keep(chunk, g, pair, values):
+        at = pl.ds((g * SUB + pair) * 2 * SUB, 2 * SUB)
+        for s, value in enumerate(values):
+            high, low = split_bf16(value)
+            bh_ref[chunk, at, s * LANES : (s + 1) * LANES] = high
+            bl_ref[chunk, at, s * LANES : (s + 1) * LANES] = low
+
+    dims = (((1,), (1,)), ((), ()))
+
+    def transform(k, place, chunk, groups):
+        at = pl.ds(groups[0] * LANES, len(groups) * LANES)
+        th, tl, bh, bl = th_ref[chunk], tl_ref[chunk], bh_ref[chunk, at, :], bl_ref[chunk, at, :]
+        res = lax.dot_general(th, bh, dims, preferred_element_type=jnp.float32)
+        res += lax.dot_general(th, bl, dims, preferred_element_type=jnp.float32)
+        res += lax.dot_general(tl, bh, dims, preferred_element_type=jnp.float32)
+        for e in range(n_devices):
+            for n, g in enumerate(groups):
+                sends[k][pl.ds(e * rows[k] + (place * RADIX + g) * SUB, SUB), :] = (
+                    res[e * SUB : (e + 1) * SUB, n * LANES : (n + 1) * LANES])
+
+    for g in range(RADIX):
+        wait_rows(x_ref, SUB * span, load_sem.at[g])
+        for pair in range(SUB):
+            keep(0, g, pair, [
+                jnp.concatenate([(a + c) + (b + d) for a, b, c, d in zip(*[rows_of(g, pair, ct, s) for ct in range(RADIX)])], 0)
+                for s in range(2)])
+        if g == 0:
+            for load in rest:
+                load.wait()
+        if g % 2:
+            transform(0, 0, 0, (g - 1, g))
+    pl.semaphore_wait(barrier, len(peers))
+    send(0)
+
     zero = jnp.zeros((SUB, LANES), jnp.float32)
     squares, zr, zi = [zero] * 4, zero, zero
     for g in range(RADIX):
-        wait_rows(x_ref, SUB * span, load_sem.at[g])
         for pair in range(SUB):
-            part = [[[x_ref[pl.ds(g * SUB * q_rows + (2 * pair + w) * SUB + 2 * ct + s, SUB, stride=q_rows), :]
-                      for w in range(2)] for s in range(2)] for ct in range(RADIX)]
+            part = [[rows_of(g, pair, ct, s) for s in range(2)] for ct in range(RADIX)]
             for ct in range(RADIX):
                 for s in range(2):
                     for w in range(2):
@@ -145,18 +189,11 @@
                 zi = zi + (part[0][1][w] * cw - part[0][0][w] * sw)
             (x0r, x0i), (x1r, x1i), (x2r, x2i), (x3r, x3i) = [
                 [jnp.concatenate(part[ct][s], 0) for s in range(2)] for ct in range(RADIX)]
-            ar, ai, br, bi = x0r + x2r, x0i + x2i, x0r - x2r, x0i - x2i
-            cr_, ci_, dr, di = x1r + x3r, x1i + x3i, x1r - x3r, x1i - x3i
-            mixed = [(ar + cr_, ai + ci_), (br - di, bi + dr), (ar - cr_, ai - ci_), (br + di, bi - dr)]
-            at = pl.ds((g * SUB + pair) * 2 * SUB, 2 * SUB)
-            for chunk in range(RADIX):
-                for s in range(2):
-                    high, low = split_bf16(mixed[chunk][s])
-                    bh_ref[chunk, at, s * LANES : (s + 1) * LANES] = high
-                    bl_ref[chunk, at, s * LANES : (s + 1) * LANES] = low
-
-    for load in rest:
-        load.wait()
+            br, bi, dr, di = x0r - x2r, x0i - x2i, x1r - x3r, x1i - x3i
+            keep(1, g, pair, (br - di, bi + dr))
+            keep(2, g, pair, ((x0r + x2r) - (x1r + x3r), (x0i + x2i) - (x1i + x3i)))
+            keep(3, g, pair, (br + di, bi - dr))
+
     pc, ps = turn_ref[2 * n_devices : 2 * n_devices + SUB, :], turn_ref[2 * n_devices + SUB :, :]
     oc, os_ = turn_ref[pl.ds(slot, 1), :], turn_ref[pl.ds(n_devices + slot, 1), :]
     total = jnp.sum(jnp.sum((squares[0] + squares[1]) + (squares[2] + squares[3]), 0, keepdims=True), 1, keepdims=True)
@@ -166,28 +203,18 @@
     wi = jnp.sum(yi * oc - yr * os_, 1, keepdims=True)
     lane = lax.broadcasted_iota(jnp.int32, (1, LANES), 1)
     stat = jnp.where(lane == 0, total, jnp.where(lane == 1, wr, jnp.where(lane == 2, wi, 0.0)))
-    sends[0][pl.ds(rows[0] - 1, n_devices, stride=rows[0]), :] = jnp.broadcast_to(stat, (n_devices, LANES))
-
-    dims = (((1,), (1,)), ((), ()))
-    for k, chunks in enumerate(PIECES):
+    sends[STAT][pl.ds(rows[STAT] - 1, n_devices, stride=rows[STAT]), :] = jnp.broadcast_to(stat, (n_devices, LANES))
+
+    for k, chunks in list(enumerate(PIECES))[1:]:
         for place, chunk in enumerate(chunks):
-            th, tl, bh, bl = th_ref[chunk], tl_ref[chunk], bh_ref[chunk], bl_ref[chunk]
-            res = lax.dot_general(th, bh, dims, preferred_element_type=jnp.float32)
-            res += lax.dot_general(th, bl, dims, preferred_element_type=jnp.float32)
-            res += lax.dot_general(tl, bh, dims, preferred_element_type=jnp.float32)
-            for e in range(n_devices):
-                for g in range(RADIX):
-                    sends[k][pl.ds(e * rows[k] + (place * RADIX + g) * SUB, SUB), :] = (
-                        res[e * SUB : (e + 1) * SUB, g * LANES : (g + 1) * LANES])
-        if k == 0:
-            pl.semaphore_wait(barrier, len(peers))
+            transform(k, place, chunk, range(RADIX))
         send(k)
 
     for k, chunks in enumerate(PIECES):
         wait_rows(recvs[k], len(peers) * rows[k], recv_sem.at[k])
         own_copy(k).wait()
-        if k == 0:
-            sums = jnp.sum(recvs[0][pl.ds(rows[0] - 1, n_devices, stride=pitches[0]), :], 0, keepdims=True)
+        if k == STAT:
+            sums = jnp.sum(recvs[k][pl.ds(rows[k] - 1, n_devices, stride=pitches[k]), :], 0, keepdims=True)
             mean_square = jnp.sum(jnp.where(lane == 0, sums, 0.0), 1, keepdims=True) / total_len
             shifted = mean_square + 1e-06
             factor = lax.rsqrt(shifted)
@@ -196,13 +223,13 @@
             tot_ref[...] = jnp.broadcast_to(checks, (SUB, LANES))
             factor = jnp.broadcast_to(factor, (SUB, LANES))
             fac_ref[...] = factor
-        if k == n_pieces - 1:
-            break
-        for place, chunk in enumerate(chunks):
-            for h in range(SUB):
-                base = ((h // 2) * (RADIX - 1) + chunk) * 2 * LANES + h % 2
-                for m, v in enumerate(turn_tiles(recvs[k], pitches[k], place, h, n_devices, factor)):
-                    field[pl.ds(base + rev(m, 4) * 2 * SUB, SUB, stride=2), :] = v
+        ready = range(STAT + 1) if k == STAT else [k] if STAT < k < n_pieces - 1 else []
+        for kk in ready:
+            for place, chunk in enumerate(PIECES[kk]):
+                for h in range(SUB):
+                    base = ((h // 2) * (RADIX - 1) + chunk) * 2 * LANES + h % 2
+                    for m, v in enumerate(turn_tiles(recvs[kk], pitches[kk], place, h, n_devices, factor)):
+                        field[pl.ds(base + rev(m, 4) * 2 * SUB, SUB, stride=2), :] = v
     for k in range(n_pieces):
         wait_rows(sends[k], len(peers) * rows[k], send_sem)
 

time: 57.1 us -> 54.6 us (0.956); the launches traced: 57 us -> 53.8 us
  Pallas kernels: 56.4 us -> 53.1 us
    pallas_call x1, Pallas kernels: 54.5 us -> 51.2 us  [fast(): pl.pallas_call(functools.partial(kernel, n_outer, n_inner, total_len), ou...]
where the time goes in v3:
time: 54.6 us; the launch traced here: 53.8 us
  Pallas kernels  53.1 us (97%)
  between operations  0.64 us (1%)
    pallas_call x1, Pallas kernels, fast(): pl.pallas_call(functools.partial(kernel, n_outer, n_inner, total_len), ou...  51.2 us
    pallas_call x1, Pallas kernels, fast(): pl.pallas_call(functools.partial(finish_kernel, n_devices, pitches[-1]),...  1.9 us

profile of v3, /device:TPU:0, one launch (start us, length us, event | category | flops | bytes accessed | tf_op | source)
XLA Modules:
  0.0 53.8 jit_solution(12891008790210479507)
XLA Ops:
  0.6 51.2 %shard_map.59 = (f32[3072,128]{1,0:T(8,128)S(1)}, f32[1152,128]{1,0:T(8,128)S(1)}, f32[8,128]{1,0:T(8,128)S(1)}, f32[8,128]{1,0:T(8,128)S(1)}) custom-call(f32[4096,128]{1,0:T(8,128)} %bitcast.11, bf16[4,256,256]{2,1,0:T(8,128)(2,1)} %constant.6.clone.th_hbm, bf16[4,256,256]{2,1,0:T(8,128)(2,1)} %constant.7.clone.tl_hbm, f32[80,128]{1,0:T(8,128)} %constant.8.clone.turn_hbm), custom_call_target="tpu_custom_call" | custom-call | tf_op jit(solution)/shard_map/pallas_call | solution.py:289
  51.9 1.9 %shard_map.60 = (f32[4096,128]{1,0:T(8,128)}, f32[1,3]{1,0:T(1,128)}) custom-call(f32[3072,128]{1,0:T(8,128)S(1)} %get-tuple-element.8.field, f32[1152,128]{1,0:T(8,128)S(1)} %get-tuple-element.9.last, f32[8,128]{1,0:T(8,128)S(1)} %get-tuple-element.10.tot_ref, f32[8,128]{1,0:T(8,128)S(1)} %get-tuple-element.11.fac_ref), custom_call_target="tpu_custom_call" | custom-call | tf_op jit(solution)/shard_map/pallas_call | solution.py:302

commit v4 on v3

--- a/solution.py
+++ b/solution.py
@@ -64,7 +64,7 @@
     n_pieces = len(PIECES)
     field, last, tot_ref, fac_ref, x_ref, th_ref, tl_ref, turn_ref, bh_ref, bl_ref = refs[:10]
     sends, recvs = refs[10 : 10 + n_pieces], [*refs[10 + n_pieces : 9 + 2 * n_pieces], last]
-    send_sem, recv_sem, own_sem, load_sem = refs[9 + 2 * n_pieces :]
+    send_sem, recv_sem, own_sem, load_sem, second_sem, third_sem = refs[9 + 2 * n_pieces :]
     n_devices = n_outer * n_inner
     obits, ibits = n_outer.bit_length() - 1, n_inner.bit_length() - 1
     span = LANES
@@ -104,28 +104,53 @@
                 pi = pi + idelta[k]
         return po, pi
 
-    half = n_inner // 2
-    high = i // half
-    far = []
-    for t in range(half):
-        pi = high * t + (1 - high) * (n_inner - 1 - t)
-        far += [(peer(mo, 0)[0], pi) for mo in range(n_outer)]
-    near = [peer(mo, mi) for mi in range(half - 1, -1, -1) for mo in range(n_outer) if mo or mi]
-    peers = [p for pair in itertools.zip_longest(far, near) for p in pair if p is not None]
+    wide = n_inner // 4
+    level, place_in = i // wide, i % wide
+    high = level // 2
+    across = level + 1 - 2 * (level % 2)
+    group = n_outer * wide
+
+    def members(at):
+        return [(peer(mo, 0)[0], at * wide + lax.rem(place_in + t, wide)) for t in range(wide) for mo in range(n_outer)]
+
+    def pairs(far, near):
+        return [p for pair in itertools.zip_longest(far, near) for p in pair if p is not None]
+
+    own = members(level)[1:]
+    first = pairs(members(2 - high), own) + members((1 - high) * across)
+    second = members(high * across + (1 - high) * 3)
+    order = pairs(members((1 - high) * 3) + members(2 - high), own + members(across))
+
     barrier = pltpu.get_barrier_semaphore()
-    for p in peers:
-        pl.semaphore_signal(barrier, inc=1, device_id=p, device_id_type=MESH)
+
+    def greet(ring, at, who=None):
+        for p in members(at) if who is None else who:
+            pl.semaphore_signal(ring, inc=1, device_id=p, device_id_type=MESH)
+
+    greet(barrier, level, own)
+    for later in range(1, 4):
+        pl.when((level < later) & (later > 1) | (high == 0) & (later == 1))(
+            functools.partial(greet, barrier, across if later == 1 else later))
+
+    def meet():
+        pl.semaphore_wait(barrier, group - 1 + jnp.where(high == 0, group, level * group))
+        for later, sem in ((2, second_sem), (3, third_sem)):
+            for earlier in range(later):
+                pl.when(level == later)(functools.partial(greet, sem, earlier))
+        pl.when(high == 0)(lambda: pl.semaphore_wait(second_sem, group))
+
+    def meet_last():
+        pl.when(level < 3)(lambda: pl.semaphore_wait(third_sem, group))
 
     rows, pitches = pieces_of(n_devices)
 
-    def send(k):
+    def send(k, peers):
         dst = recvs[k].at[pl.ds(slot * pitches[k], rows[k])]
         for po, pi in peers:
             pltpu.make_async_remote_copy(
                 src_ref=sends[k].at[pl.ds((po * n_inner + pi) * rows[k], rows[k])], dst_ref=dst,
                 send_sem=send_sem, recv_sem=recv_sem.at[k],
                 device_id=(po, pi), device_id_type=MESH).start()
-        own_copy(k).start()
 
     def own_copy(k):
         return pltpu.make_async_copy(
@@ -170,8 +195,11 @@
                 load.wait()
         if g % 2:
             transform(0, 0, 0, (g - 1, g))
-    pl.semaphore_wait(barrier, len(peers))
-    send(0)
+    meet()
+    send(0, first)
+    meet_last()
+    send(0, second)
+    own_copy(0).start()
 
     zero = jnp.zeros((SUB, LANES), jnp.float32)
     squares, zr, zi = [zero] * 4, zero, zero
@@ -208,10 +236,11 @@
     for k, chunks in list(enumerate(PIECES))[1:]:
         for place, chunk in enumerate(chunks):
             transform(k, place, chunk, range(RADIX))
-        send(k)
+        send(k, order)
+        own_copy(k).start()
 
     for k, chunks in enumerate(PIECES):
-        wait_rows(recvs[k], len(peers) * rows[k], recv_sem.at[k])
+        wait_rows(recvs[k], (n_devices - 1) * rows[k], recv_sem.at[k])
         own_copy(k).wait()
         if k == STAT:
             sums = jnp.sum(recvs[k][pl.ds(rows[k] - 1, n_devices, stride=pitches[k]), :], 0, keepdims=True)
@@ -231,10 +260,10 @@
                     for m, v in enumerate(turn_tiles(recvs[kk], pitches[kk], place, h, n_devices, factor)):
                         field[pl.ds(base + rev(m, 4) * 2 * SUB, SUB, stride=2), :] = v
     for k in range(n_pieces):
-        wait_rows(sends[k], len(peers) * rows[k], send_sem)
-
-
-def finish_kernel(n_devices, pitch, field, last, tot_ref, fac_ref, out_hbm, checks_ref, turned, sem):
+        wait_rows(sends[k], (n_devices - 1) * rows[k], send_sem)
+
+
+def finish_kernel(n_devices, pitch, field, last, tot_ref, fac_ref, out_hbm, checks_hbm, turned, checks_ref, sem):
     f_rows = 2 * LANES
     many = (RADIX - 1) * f_rows
     stores = []
@@ -243,6 +272,8 @@
             field.at[pl.ds(fq * many, many)], out_hbm.at[pl.ds(fq * RADIX * f_rows, many)], sem.at[fq]))
         stores[-1].start()
     checks_ref[...] = tot_ref[0:1, 0:3]
+    stores.append(pltpu.make_async_copy(checks_ref, checks_hbm, sem.at[2 * RADIX]))
+    stores[-1].start()
     factor = fac_ref[...]
     for h in range(SUB):
         base = h // 2 * f_rows + h % 2
@@ -285,6 +316,8 @@
         pltpu.SemaphoreType.DMA((len(PIECES),)),
         pltpu.SemaphoreType.DMA((len(PIECES),)),
         pltpu.SemaphoreType.DMA((RADIX + 3,)),
+        pltpu.SemaphoreType.REGULAR,
+        pltpu.SemaphoreType.REGULAR,
     ]
     parts = pl.pallas_call(
         functools.partial(kernel, n_outer, n_inner, total_len),
@@ -303,10 +336,11 @@
         functools.partial(finish_kernel, n_devices, pitches[-1]),
         out_shape=(jax.ShapeDtypeStruct(view.shape, jnp.float32), jax.ShapeDtypeStruct((1, 3), jnp.float32)),
         in_specs=[vmem] * 4,
-        out_specs=(hbm, vmem),
+        out_specs=(hbm, hbm),
         scratch_shapes=[
             pltpu.VMEM((RADIX * f_rows, LANES), jnp.float32),
-            pltpu.SemaphoreType.DMA((2 * RADIX,)),
+            pltpu.VMEM((1, 3), jnp.float32),
+            pltpu.SemaphoreType.DMA((2 * RADIX + 1,)),
         ],
         compiler_params=pltpu.CompilerParams(vmem_limit_bytes=32_000_000),
     )(*parts)
@@ -399,7 +433,7 @@
     def body(amplitudes):
         rows_count = amplitudes.shape[1] // COLUMNS
         n_devices = n_outer * n_inner
-        if rows_count * n_devices == LANES * LANES and n_devices * SUB == 2 * LANES:
+        if rows_count * n_devices == LANES * LANES and n_devices * SUB == 2 * LANES and n_inner % 4 == 0:
             return fast(n_outer, n_inner, amplitudes)
         return per_device(amplitudes)
 

time: 54.6 us -> 55.4 us (1.015)
  Pallas kernels: 53.1 us -> 54.1 us
    pallas_call x1, Pallas kernels: 51.2 us -> 52.7 us  [fast(): pl.pallas_call(functools.partial(kernel, n_outer, n_inner, total_len), ou...]
where the time goes in v4:
time: 55.4 us; the launch traced here: 54.7 us
  Pallas kernels  54.1 us (98%)
  between operations  0.64 us (1%)
    pallas_call x1, Pallas kernels, fast(): pl.pallas_call(functools.partial(kernel, n_outer, n_inner, total_len), ou...  52.7 us
    pallas_call x1, Pallas kernels, fast(): pl.pallas_call(functools.partial(finish_kernel, n_devices, pitches[-1]),...  1.39 us

profile of v4, /device:TPU:0, one launch (start us, length us, event | category | flops | bytes accessed | tf_op | source)
XLA Modules:
  0.0 54.7 jit_solution(8049711780191642142)
XLA Ops:
  0.6 52.7 %shard_map.59 = (f32[3072,128]{1,0:T(8,128)S(1)}, f32[1152,128]{1,0:T(8,128)S(1)}, f32[8,128]{1,0:T(8,128)S(1)}, f32[8,128]{1,0:T(8,128)S(1)}) custom-call(f32[4096,128]{1,0:T(8,128)} %bitcast.11, bf16[4,256,256]{2,1,0:T(8,128)(2,1)} %constant.6.clone.th_hbm, bf16[4,256,256]{2,1,0:T(8,128)(2,1)} %constant.7.clone.tl_hbm, f32[80,128]{1,0:T(8,128)} %constant.8.clone.turn_hbm), custom_call_target="tpu_custom_call" | custom-call | tf_op jit(solution)/shard_map/pallas_call | solution.py:322
  53.3 1.4 %shard_map.60 = (f32[4096,128]{1,0:T(8,128)}, f32[1,3]{1,0:T(1,128)}) custom-call(f32[3072,128]{1,0:T(8,128)S(1)} %get-tuple-element.8.field, f32[1152,128]{1,0:T(8,128)S(1)} %get-tuple-element.9.last, f32[8,128]{1,0:T(8,128)S(1)} %get-tuple-element.10.tot_ref, f32[8,128]{1,0:T(8,128)S(1)} %get-tuple-element.11.fac_ref), custom_call_target="tpu_custom_call" | custom-call | tf_op jit(solution)/shard_map/pallas_call | solution.py:335

commit v5 on v4

--- a/solution.py
+++ b/solution.py
@@ -64,7 +64,7 @@
     n_pieces = len(PIECES)
     field, last, tot_ref, fac_ref, x_ref, th_ref, tl_ref, turn_ref, bh_ref, bl_ref = refs[:10]
     sends, recvs = refs[10 : 10 + n_pieces], [*refs[10 + n_pieces : 9 + 2 * n_pieces], last]
-    send_sem, recv_sem, own_sem, load_sem, second_sem, third_sem = refs[9 + 2 * n_pieces :]
+    send_sem, recv_sem, own_sem, load_sem, last_sem = refs[9 + 2 * n_pieces :]
     n_devices = n_outer * n_inner
     obits, ibits = n_outer.bit_length() - 1, n_inner.bit_length() - 1
     span = LANES
@@ -128,19 +128,16 @@
             pl.semaphore_signal(ring, inc=1, device_id=p, device_id_type=MESH)
 
     greet(barrier, level, own)
-    for later in range(1, 4):
-        pl.when((level < later) & (later > 1) | (high == 0) & (later == 1))(
-            functools.partial(greet, barrier, across if later == 1 else later))
+    for t in range(1, 4):
+        pl.when(level < 3)(functools.partial(greet, barrier, lax.rem(level + t, 4)))
 
     def meet():
-        pl.semaphore_wait(barrier, group - 1 + jnp.where(high == 0, group, level * group))
-        for later, sem in ((2, second_sem), (3, third_sem)):
-            for earlier in range(later):
-                pl.when(level == later)(functools.partial(greet, sem, earlier))
-        pl.when(high == 0)(lambda: pl.semaphore_wait(second_sem, group))
+        pl.semaphore_wait(barrier, 3 * group - 1 + group * (level // 3))
+        for earlier in (2, 1, 0):
+            pl.when(level == 3)(functools.partial(greet, last_sem, earlier))
 
     def meet_last():
-        pl.when(level < 3)(lambda: pl.semaphore_wait(third_sem, group))
+        pl.when(level < 3)(lambda: pl.semaphore_wait(last_sem, group))
 
     rows, pitches = pieces_of(n_devices)
 
@@ -197,8 +194,6 @@
             transform(0, 0, 0, (g - 1, g))
     meet()
     send(0, first)
-    meet_last()
-    send(0, second)
     own_copy(0).start()
 
     zero = jnp.zeros((SUB, LANES), jnp.float32)
@@ -236,6 +231,9 @@
     for k, chunks in list(enumerate(PIECES))[1:]:
         for place, chunk in enumerate(chunks):
             transform(k, place, chunk, range(RADIX))
+        if k == 1:
+            meet_last()
+            send(0, second)
         send(k, order)
         own_copy(k).start()
 
@@ -316,7 +314,6 @@
         pltpu.SemaphoreType.DMA((len(PIECES),)),
         pltpu.SemaphoreType.DMA((len(PIECES),)),
         pltpu.SemaphoreType.DMA((RADIX + 3,)),
-        pltpu.SemaphoreType.REGULAR,
         pltpu.SemaphoreType.REGULAR,
     ]
     parts = pl.pallas_call(

time: 55.4 us -> 54.7 us (0.987); the launches traced: 54.7 us -> 54.6 us
  no operation moved by 1% of the time
where the time goes in v5:
time: 54.7 us; the launch traced here: 54.6 us
  Pallas kernels  53.9 us (99%)
  between operations  0.64 us (1%)
    pallas_call x1, Pallas kernels, fast(): pl.pallas_call(functools.partial(kernel, n_outer, n_inner, total_len), ou...  52.5 us
    pallas_call x1, Pallas kernels, fast(): pl.pallas_call(functools.partial(finish_kernel, n_devices, pitches[-1]),...  1.39 us

profile of v5, /device:TPU:0, one launch (start us, length us, event | category | flops | bytes accessed | tf_op | source)
XLA Modules:
  0.0 54.6 jit_solution(2446871960637652737)
XLA Ops:
  0.6 52.5 %shard_map.59 = (f32[3072,128]{1,0:T(8,128)S(1)}, f32[1152,128]{1,0:T(8,128)S(1)}, f32[8,128]{1,0:T(8,128)S(1)}, f32[8,128]{1,0:T(8,128)S(1)}) custom-call(f32[4096,128]{1,0:T(8,128)} %bitcast.11, bf16[4,256,256]{2,1,0:T(8,128)(2,1)} %constant.6.clone.th_hbm, bf16[4,256,256]{2,1,0:T(8,128)(2,1)} %constant.7.clone.tl_hbm, f32[80,128]{1,0:T(8,128)} %constant.8.clone.turn_hbm), custom_call_target="tpu_custom_call" | custom-call | tf_op jit(solution)/shard_map/pallas_call | solution.py:319
  53.2 1.4 %shard_map.60 = (f32[4096,128]{1,0:T(8,128)}, f32[1,3]{1,0:T(1,128)}) custom-call(f32[3072,128]{1,0:T(8,128)S(1)} %get-tuple-element.8.field, f32[1152,128]{1,0:T(8,128)S(1)} %get-tuple-element.9.last, f32[8,128]{1,0:T(8,128)S(1)} %get-tuple-element.10.tot_ref, f32[8,128]{1,0:T(8,128)S(1)} %get-tuple-element.11.fac_ref), custom_call_target="tpu_custom_call" | custom-call | tf_op jit(solution)/shard_map/pallas_call | solution.py:332

commit v6 on v5

--- a/solution.py
+++ b/solution.py
@@ -113,13 +113,16 @@
     def members(at):
         return [(peer(mo, 0)[0], at * wide + lax.rem(place_in + t, wide)) for t in range(wide) for mo in range(n_outer)]
 
+    def ranked(at):
+        return [(o2 + c, at * wide + t) for o2 in range(0, n_outer, 2) for t in range(wide) for c in range(2)]
+
     def pairs(far, near):
         return [p for pair in itertools.zip_longest(far, near) for p in pair if p is not None]
 
     own = members(level)[1:]
-    first = pairs(members(2 - high), own) + members((1 - high) * across)
-    second = members(high * across + (1 - high) * 3)
-    order = pairs(members((1 - high) * 3) + members(2 - high), own + members(across))
+    first = pairs(ranked(2 - high), own) + members((1 - high) * across)
+    second = ranked(high * across + (1 - high) * 3)
+    order = pairs(ranked((1 - high) * 3) + ranked(2 - high), own + members(across))
 
     barrier = pltpu.get_barrier_semaphore()
 

time: 54.7 us -> 53.3 us (0.974); the launches traced: 54.6 us -> 52.5 us
  Pallas kernels: 53.9 us -> 51.8 us
    pallas_call x1, Pallas kernels: 52.5 us -> 50.4 us  [fast(): pl.pallas_call(functools.partial(kernel, n_outer, n_inner, total_len), ou...]
where the time goes in v6:
time: 53.3 us; the launch traced here: 52.5 us
  Pallas kernels  51.8 us (97%)
  between operations  0.64 us (1%)
    pallas_call x1, Pallas kernels, fast(): pl.pallas_call(functools.partial(kernel, n_outer, n_inner, total_len), ou...  50.4 us
    pallas_call x1, Pallas kernels, fast(): pl.pallas_call(functools.partial(finish_kernel, n_devices, pitches[-1]),...  1.39 us

profile of v6, /device:TPU:0, one launch (start us, length us, event | category | flops | bytes accessed | tf_op | source)
XLA Modules:
  0.0 52.5 jit_solution(7035621069580359422)
XLA Ops:
  0.6 50.4 %shard_map.59 = (f32[3072,128]{1,0:T(8,128)S(1)}, f32[1152,128]{1,0:T(8,128)S(1)}, f32[8,128]{1,0:T(8,128)S(1)}, f32[8,128]{1,0:T(8,128)S(1)}) custom-call(f32[4096,128]{1,0:T(8,128)} %bitcast.11, bf16[4,256,256]{2,1,0:T(8,128)(2,1)} %constant.6.clone.th_hbm, bf16[4,256,256]{2,1,0:T(8,128)(2,1)} %constant.7.clone.tl_hbm, f32[80,128]{1,0:T(8,128)} %constant.8.clone.turn_hbm), custom_call_target="tpu_custom_call" | custom-call | tf_op jit(solution)/shard_map/pallas_call | solution.py:322
  51.1 1.4 %shard_map.60 = (f32[4096,128]{1,0:T(8,128)}, f32[1,3]{1,0:T(1,128)}) custom-call(f32[3072,128]{1,0:T(8,128)S(1)} %get-tuple-element.8.field, f32[1152,128]{1,0:T(8,128)S(1)} %get-tuple-element.9.last, f32[8,128]{1,0:T(8,128)S(1)} %get-tuple-element.10.tot_ref, f32[8,128]{1,0:T(8,128)S(1)} %get-tuple-element.11.fac_ref), custom_call_target="tpu_custom_call" | custom-call | tf_op jit(solution)/shard_map/pallas_call | solution.py:335

commit v7 on v6

--- a/solution.py
+++ b/solution.py
@@ -49,8 +49,8 @@
 
 
 def pieces_of(n_devices):
-    rows = [len(chunks) * RADIX * SUB + (k == STAT) for k, chunks in enumerate(PIECES)]
-    return rows, [r if r % 2 else r + 4 for r in rows]
+    rows = [len(chunks) * RADIX * SUB for chunks in PIECES]
+    return rows, [r + 4 for r in rows]
 
 
 def turn_tiles(recv, pitch, place, h, n_devices, factor):
@@ -64,7 +64,7 @@
     n_pieces = len(PIECES)
     field, last, tot_ref, fac_ref, x_ref, th_ref, tl_ref, turn_ref, bh_ref, bl_ref = refs[:10]
     sends, recvs = refs[10 : 10 + n_pieces], [*refs[10 + n_pieces : 9 + 2 * n_pieces], last]
-    send_sem, recv_sem, own_sem, load_sem, last_sem = refs[9 + 2 * n_pieces :]
+    near_ref, half_ref, far_ref, send_sem, recv_sem, own_sem, load_sem, last_sem, stat_sem = refs[9 + 2 * n_pieces :]
     n_devices = n_outer * n_inner
     obits, ibits = n_outer.bit_length() - 1, n_inner.bit_length() - 1
     span = LANES
@@ -76,9 +76,11 @@
             loads.append(pltpu.make_async_copy(
                 x_hbm.at[pl.ds((g * SUB + q) * span, span)],
                 x_ref.at[pl.ds((g * SUB + rev(q, 3)) * q_rows, span)], load_sem.at[g]))
-    rest = [pltpu.make_async_copy(src, dst, load_sem.at[RADIX + k]) for k, (src, dst) in enumerate(
-        [(th_hbm, th_ref), (tl_hbm, tl_ref), (turn_hbm, turn_ref)])]
-    for load in loads + rest:
+    head = [pltpu.make_async_copy(src.at[0], dst.at[0], load_sem.at[RADIX]) for src, dst in ((th_hbm, th_ref), (tl_hbm, tl_ref))]
+    rest = [pltpu.make_async_copy(src.at[pl.ds(1, RADIX - 1)], dst.at[pl.ds(1, RADIX - 1)], load_sem.at[RADIX + 1])
+            for src, dst in ((th_hbm, th_ref), (tl_hbm, tl_ref))]
+    rest.append(pltpu.make_async_copy(turn_hbm, turn_ref, load_sem.at[RADIX + 2]))
+    for load in loads[: 2 * SUB] + head:
         load.start()
 
     o, i = lax.axis_index("outer"), lax.axis_index("inner")
@@ -106,6 +108,7 @@
 
     wide = n_inner // 4
     level, place_in = i // wide, i % wide
+    half = n_inner // 2
     high = level // 2
     across = level + 1 - 2 * (level % 2)
     group = n_outer * wide
@@ -130,12 +133,16 @@
         for p in members(at) if who is None else who:
             pl.semaphore_signal(ring, inc=1, device_id=p, device_id_type=MESH)
 
+    for at in (2 - high, (1 - high) * 3, across):
+        pl.when(level < 3)(functools.partial(greet, barrier, at))
     greet(barrier, level, own)
-    for t in range(1, 4):
-        pl.when(level < 3)(functools.partial(greet, barrier, lax.rem(level + t, 4)))
+    for load in loads[2 * SUB :] + rest:
+        load.start()
 
     def meet():
         pl.semaphore_wait(barrier, 3 * group - 1 + group * (level // 3))
+
+    def answer():
         for earlier in (2, 1, 0):
             pl.when(level == 3)(functools.partial(greet, last_sem, earlier))
 
@@ -190,13 +197,14 @@
             keep(0, g, pair, [
                 jnp.concatenate([(a + c) + (b + d) for a, b, c, d in zip(*[rows_of(g, pair, ct, s) for ct in range(RADIX)])], 0)
                 for s in range(2)])
-        if g == 0:
-            for load in rest:
-                load.wait()
+        if g == 1:
+            wait_rows(th_ref, 1, load_sem.at[RADIX])
+            wait_rows(tl_ref, 1, load_sem.at[RADIX])
         if g % 2:
             transform(0, 0, 0, (g - 1, g))
     meet()
     send(0, first)
+    answer()
     own_copy(0).start()
 
     zero = jnp.zeros((SUB, LANES), jnp.float32)
@@ -220,6 +228,9 @@
             keep(2, g, pair, ((x0r + x2r) - (x1r + x3r), (x0i + x2i) - (x1i + x3i)))
             keep(3, g, pair, (br + di, bi - dr))
 
+    for ref in (th_ref, tl_ref):
+        wait_rows(ref, RADIX - 1, load_sem.at[RADIX + 1])
+    rest[-1].wait()
     pc, ps = turn_ref[2 * n_devices : 2 * n_devices + SUB, :], turn_ref[2 * n_devices + SUB :, :]
     oc, os_ = turn_ref[pl.ds(slot, 1), :], turn_ref[pl.ds(n_devices + slot, 1), :]
     total = jnp.sum(jnp.sum((squares[0] + squares[1]) + (squares[2] + squares[3]), 0, keepdims=True), 1, keepdims=True)
@@ -229,7 +240,13 @@
     wi = jnp.sum(yi * oc - yr * os_, 1, keepdims=True)
     lane = lax.broadcasted_iota(jnp.int32, (1, LANES), 1)
     stat = jnp.where(lane == 0, total, jnp.where(lane == 1, wr, jnp.where(lane == 2, wi, 0.0)))
-    sends[STAT][pl.ds(rows[STAT] - 1, n_devices, stride=rows[STAT]), :] = jnp.broadcast_to(stat, (n_devices, LANES))
+    mine = pl.ds(o * half + i % half, 1)
+    near_ref[mine, :] = stat
+
+    def send_row(src, dst, sem, to):
+        pltpu.make_async_remote_copy(
+            src_ref=src, dst_ref=dst, send_sem=send_sem, recv_sem=stat_sem.at[sem],
+            device_id=to, device_id_type=MESH).start()
 
     for k, chunks in list(enumerate(PIECES))[1:]:
         for place, chunk in enumerate(chunks):
@@ -237,6 +254,12 @@
         if k == 1:
             meet_last()
             send(0, second)
+            for to in own + members(across):
+                send_row(near_ref.at[mine], near_ref.at[mine], 0, to)
+        if k == n_pieces - 1:
+            wait_rows(near_ref, half * n_outer - 1, stat_sem.at[0])
+            half_ref[...] = jnp.sum(near_ref[...], 0, keepdims=True)
+            send_row(half_ref, far_ref, 1, peer(0, half))
         send(k, order)
         own_copy(k).start()
 
@@ -244,7 +267,8 @@
         wait_rows(recvs[k], (n_devices - 1) * rows[k], recv_sem.at[k])
         own_copy(k).wait()
         if k == STAT:
-            sums = jnp.sum(recvs[k][pl.ds(rows[k] - 1, n_devices, stride=pitches[k]), :], 0, keepdims=True)
+            wait_rows(far_ref, 1, stat_sem.at[1])
+            sums = half_ref[...] + far_ref[...]
             mean_square = jnp.sum(jnp.where(lane == 0, sums, 0.0), 1, keepdims=True) / total_len
             shifted = mean_square + 1e-06
             factor = lax.rsqrt(shifted)
@@ -262,6 +286,7 @@
                         field[pl.ds(base + rev(m, 4) * 2 * SUB, SUB, stride=2), :] = v
     for k in range(n_pieces):
         wait_rows(sends[k], (n_devices - 1) * rows[k], send_sem)
+    wait_rows(near_ref, half * n_outer, send_sem)
 
 
 def finish_kernel(n_devices, pitch, field, last, tot_ref, fac_ref, out_hbm, checks_hbm, turned, checks_ref, sem):
@@ -313,11 +338,15 @@
         pair,
         *[pltpu.VMEM((n_devices * r, LANES), jnp.float32) for r in rows],
         *[pltpu.VMEM((n_devices * p, LANES), jnp.float32) for p in pitches[:-1]],
+        pltpu.VMEM((n_devices // 2, LANES), jnp.float32),
+        pltpu.VMEM((1, LANES), jnp.float32),
+        pltpu.VMEM((1, LANES), jnp.float32),
         pltpu.SemaphoreType.DMA,
         pltpu.SemaphoreType.DMA((len(PIECES),)),
         pltpu.SemaphoreType.DMA((len(PIECES),)),
         pltpu.SemaphoreType.DMA((RADIX + 3,)),
         pltpu.SemaphoreType.REGULAR,
+        pltpu.SemaphoreType.DMA((2,)),
     ]
     parts = pl.pallas_call(
         functools.partial(kernel, n_outer, n_inner, total_len),

time: 53.3 us -> 52.6 us (0.987)
  the two profiles are of different devices: /device:TPU:0 before, /device:TPU:15 now
where the time goes in v7:
time: 52.6 us; the launch traced here: 52.5 us
  Pallas kernels  51.8 us (98%)
  between operations  0.64 us (1%)
    pallas_call x1, Pallas kernels, fast(): pl.pallas_call(functools.partial(kernel, n_outer, n_inner, total_len), ou...  50.5 us
    pallas_call x1, Pallas kernels, fast(): pl.pallas_call(functools.partial(finish_kernel, n_devices, pitches[-1]),...  1.39 us

profile of v7, /device:TPU:15, one launch (start us, length us, event | category | flops | bytes accessed | tf_op | source)
XLA Modules:
  0.0 52.5 jit_solution(9061594341147659201)
XLA Ops:
  0.6 50.5 %shard_map.59 = (f32[3072,128]{1,0:T(8,128)S(1)}, f32[1152,128]{1,0:T(8,128)S(1)}, f32[8,128]{1,0:T(8,128)S(1)}, f32[8,128]{1,0:T(8,128)S(1)}) custom-call(f32[4096,128]{1,0:T(8,128)} %bitcast.11, bf16[4,256,256]{2,1,0:T(8,128)(2,1)} %constant.6.clone.th_hbm, bf16[4,256,256]{2,1,0:T(8,128)(2,1)} %constant.7.clone.tl_hbm, f32[80,128]{1,0:T(8,128)} %constant.8.clone.turn_hbm), custom_call_target="tpu_custom_call" | custom-call | tf_op jit(solution)/shard_map/pallas_call | solution.py:351
  51.1 1.4 %shard_map.60 = (f32[4096,128]{1,0:T(8,128)}, f32[1,3]{1,0:T(1,128)}) custom-call(f32[3072,128]{1,0:T(8,128)S(1)} %get-tuple-element.8.field, f32[1152,128]{1,0:T(8,128)S(1)} %get-tuple-element.9.last, f32[8,128]{1,0:T(8,128)S(1)} %get-tuple-element.10.tot_ref, f32[8,128]{1,0:T(8,128)S(1)} %get-tuple-element.11.fac_ref), custom_call_target="tpu_custom_call" | custom-call | tf_op jit(solution)/shard_map/pallas_call | solution.py:364

commit v8 on v7

--- a/solution.py
+++ b/solution.py
@@ -123,9 +123,11 @@
         return [p for pair in itertools.zip_longest(far, near) for p in pair if p is not None]
 
     own = members(level)[1:]
-    first = pairs(ranked(2 - high), own) + members((1 - high) * across)
-    second = ranked(high * across + (1 - high) * 3)
-    order = pairs(ranked((1 - high) * 3) + ranked(2 - high), own + members(across))
+    first = ranked(2 - high)[:-2]
+    then = members((1 - high) * across)
+    second = ranked(2 - high)[-2:] + pairs(ranked(high * across + (1 - high) * 3), own)
+    order = ranked((1 - high) * 3) + ranked(2 - high) + own + members(across)
+    left = pairs(ranked((1 - high) * 3) + ranked(2 - high)[-2:], own + members(across))
 
     barrier = pltpu.get_barrier_semaphore()
 
@@ -133,21 +135,25 @@
         for p in members(at) if who is None else who:
             pl.semaphore_signal(ring, inc=1, device_id=p, device_id_type=MESH)
 
+    tail = ranked(2)[-2:] + ranked(3)
+    late = (level == 3) | (level == 2) & (o >= n_outer - 2) & (place_in == wide - 1)
     for at in (2 - high, (1 - high) * 3, across):
-        pl.when(level < 3)(functools.partial(greet, barrier, at))
-    greet(barrier, level, own)
+        pl.when(~late)(functools.partial(greet, barrier, at))
+    pl.when(~late)(functools.partial(greet, barrier, level, own))
+    for p in tail:
+        pl.when(late & ((p[0] != o) | (p[1] != i)))(functools.partial(greet, barrier, level, [p]))
     for load in loads[2 * SUB :] + rest:
         load.start()
 
     def meet():
-        pl.semaphore_wait(barrier, 3 * group - 1 + group * (level // 3))
+        pl.semaphore_wait(barrier, n_devices - 1 - len(tail) + len(tail) * late.astype(jnp.int32))
 
     def answer():
-        for earlier in (2, 1, 0):
-            pl.when(level == 3)(functools.partial(greet, last_sem, earlier))
+        for p in ranked(0) + ranked(1) + ranked(2)[:-2]:
+            pl.when(late)(functools.partial(greet, last_sem, level, [p]))
 
     def meet_last():
-        pl.when(level < 3)(lambda: pl.semaphore_wait(last_sem, group))
+        pl.when(~late)(lambda: pl.semaphore_wait(last_sem, len(tail)))
 
     rows, pitches = pieces_of(n_devices)
 
@@ -180,16 +186,23 @@
 
     dims = (((1,), (1,)), ((), ()))
 
-    def transform(k, place, chunk, groups):
+    def transform(k, place, chunk, groups, side=None):
         at = pl.ds(groups[0] * LANES, len(groups) * LANES)
         th, tl, bh, bl = th_ref[chunk], tl_ref[chunk], bh_ref[chunk, at, :], bl_ref[chunk, at, :]
+        starts = range(n_devices)
+        if side is not None:
+            count = half * SUB
+            heads = [o2 * n_inner + side * half for o2 in range(n_outer)]
+            th, tl = [jnp.concatenate([ref[chunk, pl.ds(pl.multiple_of(e * SUB, count), count), :] for e in heads], 0)
+                      for ref in (th_ref, tl_ref)]
+            starts = [e + n for e in heads for n in range(half)]
         res = lax.dot_general(th, bh, dims, preferred_element_type=jnp.float32)
         res += lax.dot_general(th, bl, dims, preferred_element_type=jnp.float32)
         res += lax.dot_general(tl, bh, dims, preferred_element_type=jnp.float32)
-        for e in range(n_devices):
+        for m, e in enumerate(starts):
             for n, g in enumerate(groups):
-                sends[k][pl.ds(e * rows[k] + (place * RADIX + g) * SUB, SUB), :] = (
-                    res[e * SUB : (e + 1) * SUB, n * LANES : (n + 1) * LANES])
+                sends[k][pl.ds(pl.multiple_of(e * rows[k] + (place * RADIX + g) * SUB, SUB), SUB), :] = (
+                    res[m * SUB : (m + 1) * SUB, n * LANES : (n + 1) * LANES])
 
     for g in range(RADIX):
         wait_rows(x_ref, SUB * span, load_sem.at[g])
@@ -201,10 +214,12 @@
             wait_rows(th_ref, 1, load_sem.at[RADIX])
             wait_rows(tl_ref, 1, load_sem.at[RADIX])
         if g % 2:
-            transform(0, 0, 0, (g - 1, g))
+            transform(0, 0, 0, (g - 1, g), 1 - high)
     meet()
     send(0, first)
     answer()
+    transform(0, 0, 0, range(RADIX), high)
+    send(0, then)
     own_copy(0).start()
 
     zero = jnp.zeros((SUB, LANES), jnp.float32)
@@ -252,6 +267,7 @@
         for place, chunk in enumerate(chunks):
             transform(k, place, chunk, range(RADIX))
         if k == 1:
+            send(1, first)
             meet_last()
             send(0, second)
             for to in own + members(across):
@@ -260,7 +276,7 @@
             wait_rows(near_ref, half * n_outer - 1, stat_sem.at[0])
             half_ref[...] = jnp.sum(near_ref[...], 0, keepdims=True)
             send_row(half_ref, far_ref, 1, peer(0, half))
-        send(k, order)
+        send(k, left if k == 1 else order)
         own_copy(k).start()
 
     for k, chunks in enumerate(PIECES):

time: 52.6 us -> 52.4 us (level)
  the two profiles are of different devices: /device:TPU:15 before, /device:TPU:0 now
where the time goes in v8:
time: 52.4 us; the launch traced here: 51.5 us
  Pallas kernels  50.9 us (97%)
  between operations  0.64 us (1%)
    pallas_call x1, Pallas kernels, fast(): pl.pallas_call(functools.partial(kernel, n_outer, n_inner, total_len), ou...  49.5 us
    pallas_call x1, Pallas kernels, fast(): pl.pallas_call(functools.partial(finish_kernel, n_devices, pitches[-1]),...  1.39 us

profile of v8, /device:TPU:0, one launch (start us, length us, event | category | flops | bytes accessed | tf_op | source)
XLA Modules:
  0.0 51.5 jit_solution(13501177736853366733)
XLA Ops:
  0.6 49.5 %shard_map.59 = (f32[3072,128]{1,0:T(8,128)S(1)}, f32[1152,128]{1,0:T(8,128)S(1)}, f32[8,128]{1,0:T(8,128)S(1)}, f32[8,128]{1,0:T(8,128)S(1)}) custom-call(f32[4096,128]{1,0:T(8,128)} %bitcast.11, bf16[4,256,256]{2,1,0:T(8,128)(2,1)} %constant.6.clone.th_hbm, bf16[4,256,256]{2,1,0:T(8,128)(2,1)} %constant.7.clone.tl_hbm, f32[80,128]{1,0:T(8,128)} %constant.8.clone.turn_hbm), custom_call_target="tpu_custom_call" | custom-call | tf_op jit(solution)/shard_map/pallas_call | solution.py:367
  50.2 1.4 %shard_map.60 = (f32[4096,128]{1,0:T(8,128)}, f32[1,3]{1,0:T(1,128)}) custom-call(f32[3072,128]{1,0:T(8,128)S(1)} %get-tuple-element.8.field, f32[1152,128]{1,0:T(8,128)S(1)} %get-tuple-element.9.last, f32[8,128]{1,0:T(8,128)S(1)} %get-tuple-element.10.tot_ref, f32[8,128]{1,0:T(8,128)S(1)} %get-tuple-element.11.fac_ref), custom_call_target="tpu_custom_call" | custom-call | tf_op jit(solution)/shard_map/pallas_call | solution.py:380

commit v9 on v8

--- a/solution.py
+++ b/solution.py
@@ -311,11 +311,11 @@
     stores = []
     for fq in range(RADIX):
         stores.append(pltpu.make_async_copy(
-            field.at[pl.ds(fq * many, many)], out_hbm.at[pl.ds(fq * RADIX * f_rows, many)], sem.at[fq]))
+            field.at[pl.ds(fq * many, many)], out_hbm.at[pl.ds(fq * RADIX * f_rows, many)], sem.at[0]))
         stores[-1].start()
     checks_ref[...] = tot_ref[0:1, 0:3]
-    stores.append(pltpu.make_async_copy(checks_ref, checks_hbm, sem.at[2 * RADIX]))
-    stores[-1].start()
+    checks_copy = pltpu.make_async_copy(checks_ref, checks_hbm, sem.at[1])
+    checks_copy.start()
     factor = fac_ref[...]
     for h in range(SUB):
         base = h // 2 * f_rows + h % 2
@@ -325,10 +325,10 @@
             fq = h // 2
             stores.append(pltpu.make_async_copy(
                 turned.at[pl.ds(fq * f_rows, f_rows)],
-                out_hbm.at[pl.ds((fq * RADIX + RADIX - 1) * f_rows, f_rows)], sem.at[RADIX + fq]))
+                out_hbm.at[pl.ds((fq * RADIX + RADIX - 1) * f_rows, f_rows)], sem.at[0]))
             stores[-1].start()
-    for store in stores:
-        store.wait()
+    pltpu.make_async_copy(out_hbm, out_hbm, sem.at[0]).wait()
+    checks_copy.wait()
 
 
 def fast(n_outer, n_inner, amplitudes):
@@ -385,7 +385,7 @@
         scratch_shapes=[
             pltpu.VMEM((RADIX * f_rows, LANES), jnp.float32),
             pltpu.VMEM((1, 3), jnp.float32),
-            pltpu.SemaphoreType.DMA((2 * RADIX + 1,)),
+            pltpu.SemaphoreType.DMA((2,)),
         ],
         compiler_params=pltpu.CompilerParams(vmem_limit_bytes=32_000_000),
     )(*parts)

time: 52.4 us -> 52.4 us (level)
  no operation moved by 1% of the time
where the time goes in v9:
time: 52.4 us; the launch traced here: 51.5 us
  Pallas kernels  50.8 us (97%)
  between operations  0.64 us (1%)
    pallas_call x1, Pallas kernels, fast(): pl.pallas_call(functools.partial(kernel, n_outer, n_inner, total_len), ou...  49.5 us
    pallas_call x1, Pallas kernels, fast(): pl.pallas_call(functools.partial(finish_kernel, n_devices, pitches[-1]),...  1.33 us

profile of v9, /device:TPU:0, one launch (start us, length us, event | category | flops | bytes accessed | tf_op | source)
XLA Modules:
  0.0 51.5 jit_solution(9132684851761509866)
XLA Ops:
  0.6 49.5 %shard_map.59 = (f32[3072,128]{1,0:T(8,128)S(1)}, f32[1152,128]{1,0:T(8,128)S(1)}, f32[8,128]{1,0:T(8,128)S(1)}, f32[8,128]{1,0:T(8,128)S(1)}) custom-call(f32[4096,128]{1,0:T(8,128)} %bitcast.11, bf16[4,256,256]{2,1,0:T(8,128)(2,1)} %constant.6.clone.th_hbm, bf16[4,256,256]{2,1,0:T(8,128)(2,1)} %constant.7.clone.tl_hbm, f32[80,128]{1,0:T(8,128)} %constant.8.clone.turn_hbm), custom_call_target="tpu_custom_call" | custom-call | tf_op jit(solution)/shard_map/pallas_call | solution.py:367
  50.2 1.3 %shard_map.60 = (f32[4096,128]{1,0:T(8,128)}, f32[1,3]{1,0:T(1,128)}) custom-call(f32[3072,128]{1,0:T(8,128)S(1)} %get-tuple-element.8.field, f32[1152,128]{1,0:T(8,128)S(1)} %get-tuple-element.9.last, f32[8,128]{1,0:T(8,128)S(1)} %get-tuple-element.10.tot_ref, f32[8,128]{1,0:T(8,128)S(1)} %get-tuple-element.11.fac_ref), custom_call_target="tpu_custom_call" | custom-call | tf_op jit(solution)/shard_map/pallas_call | solution.py:380
